TPU v7x, 32 devices: a 4x4x1 block of a 4x4x8 slice. The times are simulated.
32 devices in a mesh: part: 1 (over z), tpa: 4 (over y), tpb: 8 (over x, core).
Axes of the slice: x: 4, y: 4, z: 1, core: 2. Of those that a mesh axis runs over, the one named last changes fastest.
The devices are a block of a 4x4x8 slice.
Arguments:
- x: bfloat16 [8, 1024, 4096], P(('part', 'tpb'))
- lengths: int32 [8], P(('part', 'tpb'))
- k_buf: bfloat16 [8, 1024, 32, 128], P(('part', 'tpb'), None, 'tpa')
- v_buf: bfloat16 [8, 1024, 32, 128], P(('part', 'tpb'), None, 'tpa')
- w_qkv: bfloat16 [4096, 12288], P('part', ('tpa', 'tpb'))
- w_o: bfloat16 [4096, 4096], P(('part', 'tpa', 'tpb'))
- w_gate_up: bfloat16 [4096, 22016], P('part', ('tpa', 'tpb'))
- w_down: bfloat16 [11008, 4096], P(('part', 'tpa', 'tpb'))
- g_attn: bfloat16 [4096], P('part')
- g_mlp: bfloat16 [4096], P('part')
Outputs:
- output 1: bfloat16 [8, 1024, 4096], P(('part', 'tpb'))
- output 2: bfloat16 [8, 1024, 32, 128], P(('part', 'tpb'), None, 'tpa')
- output 3: bfloat16 [8, 1024, 32, 128], P(('part', 'tpb'), None, 'tpa')
- output 4: bfloat16 [4096, 4096], P('part', 'tpa')
- output 5: bfloat16 [4096, 4096], P('part', 'tpa')
- output 6: bfloat16 [4096, 4096], P('part', 'tpa')
- output 7: bfloat16 [4096, 4096], P(('part', 'tpa'))
- output 8: bfloat16 [4096, 11008], P('part', 'tpa')
- output 9: bfloat16 [4096, 11008], P('part', 'tpa')
- output 10: bfloat16 [11008, 4096], P(('part', 'tpa'))
All inputs are finite; a program needn't handle non-finite values.
Results may differ from a plain program's by a relative error of at most 0.0139058.
Values are sent between devices in bfloat16 or wider.
A program may use at most 768 MiB of HBM per device.

v0:
```python
import math
import jax
import jax.numpy as jnp
from jax import lax
from jax.sharding import PartitionSpec as P

ROPE_BASE = 500000.0
ROPE_FACTOR = 8.0
LOW_FREQ = 1.0
HIGH_FREQ = 4.0
ORIG_CONTEXT = 8192.0
NORM_EPS = 1e-5
MASK_VALUE = -1e30


def rms_norm(x_in, gain_vec):
    x_wide = x_in.astype(jnp.float32)
    mean_sq = jnp.mean(x_wide * x_wide, axis=-1, keepdims=True)
    return (x_wide * lax.rsqrt(mean_sq + NORM_EPS) * gain_vec.astype(jnp.float32)).astype(jnp.bfloat16)


def rope_tables(seq_len, head_dim):
    exponent = jnp.arange(head_dim // 2, dtype=jnp.float32) * (2.0 / head_dim)
    inv_freq = 1.0 / jnp.power(ROPE_BASE, exponent)
    wavelen = 2.0 * math.pi / inv_freq
    smooth = (ORIG_CONTEXT / wavelen - LOW_FREQ) / (HIGH_FREQ - LOW_FREQ)
    blended = (1.0 - smooth) * inv_freq / ROPE_FACTOR + smooth * inv_freq
    rope_freq = jnp.where(wavelen < ORIG_CONTEXT / HIGH_FREQ, inv_freq, jnp.where(wavelen > ORIG_CONTEXT / LOW_FREQ, inv_freq / ROPE_FACTOR, blended))
    angles = jnp.arange(seq_len, dtype=jnp.float32)[:, None] * rope_freq[None, :]
    return jnp.cos(angles), jnp.sin(angles)


def apply_rope(vec_in, cos_tab, sin_tab):
    half_dim = vec_in.shape[-1] // 2
    first_half = vec_in[..., :half_dim]
    second_half = vec_in[..., half_dim:]
    return jnp.concatenate([first_half * cos_tab - second_half * sin_tab, second_half * cos_tab + first_half * sin_tab], axis=-1)


def split_weights(qkv_cols, gu_cols, kv_local, head_dim, n_tpb):
    model_dim = qkv_cols.shape[0]
    group_size = qkv_cols.shape[1] // (kv_local * head_dim) - 2
    packed = qkv_cols.reshape(model_dim, kv_local, group_size + 2, head_dim)
    w_query = packed[:, :, :group_size, :].reshape(model_dim, kv_local * group_size * head_dim)
    w_key = packed[:, :, group_size, :].reshape(model_dim, kv_local * head_dim)
    w_value = packed[:, :, group_size + 1, :].reshape(model_dim, kv_local * head_dim)
    ff_block = gu_cols.shape[1] // (2 * n_tpb)
    gu_view = gu_cols.reshape(model_dim, n_tpb, 2, ff_block)
    w_gate = gu_view[:, :, 0, :].reshape(model_dim, n_tpb * ff_block)
    w_up = gu_view[:, :, 1, :].reshape(model_dim, n_tpb * ff_block)
    return w_query, w_key, w_value, w_gate, w_up


def prefill(x_loc, len_loc, k_buf, v_buf, qkv_cols, o_rows, gu_cols, down_rows, g_attn, g_mlp, n_tpb):
    batch_loc, seq_len, model_dim = x_loc.shape
    kv_local = k_buf.shape[2]
    head_dim = k_buf.shape[3]
    group_size = qkv_cols.shape[1] // (kv_local * head_dim) - 2
    x_normed = rms_norm(x_loc, g_attn)
    qkv_act = jnp.einsum('bsd,dc->bsc', x_normed, qkv_cols, preferred_element_type=jnp.float32).astype(jnp.bfloat16)
    qkv_act = qkv_act.reshape(batch_loc, seq_len, kv_local, group_size + 2, head_dim)
    cos_tab, sin_tab = rope_tables(seq_len, head_dim)
    q_rot = apply_rope(qkv_act[:, :, :, :group_size, :].astype(jnp.float32), cos_tab[:, None, None, :], sin_tab[:, None, None, :]).astype(jnp.bfloat16)
    k_rot = apply_rope(qkv_act[:, :, :, group_size, :].astype(jnp.float32), cos_tab[:, None, :], sin_tab[:, None, :]).astype(jnp.bfloat16)
    values = qkv_act[:, :, :, group_size + 1, :]
    scores = jnp.einsum('bqkgd,bskd->bkgqs', q_rot, k_rot, preferred_element_type=jnp.float32) * head_dim ** -0.5
    positions = jnp.arange(seq_len)
    allowed = (positions[None, None, :] <= positions[None, :, None]) & (positions[None, None, :] < len_loc[:, None, None])
    scores = jnp.where(allowed[:, None, None], scores, MASK_VALUE)
    attn_prob = jax.nn.softmax(scores, axis=-1).astype(jnp.bfloat16)
    attn_out = jnp.einsum('bkgqs,bskd->bqkgd', attn_prob, values, preferred_element_type=jnp.float32).astype(jnp.bfloat16)
    attn_out = attn_out.reshape(batch_loc, seq_len, kv_local * group_size * head_dim)
    attn_part = jnp.einsum('bsh,hd->bsd', attn_out, o_rows, preferred_element_type=jnp.float32).astype(jnp.bfloat16)
    attn_sum = lax.psum(attn_part, 'tpa')
    hidden = (x_loc.astype(jnp.float32) + attn_sum.astype(jnp.float32)).astype(jnp.bfloat16)
    h_normed = rms_norm(hidden, g_mlp)
    ff_block = gu_cols.shape[1] // (2 * n_tpb)
    gu_act = jnp.einsum('bsd,dc->bsc', h_normed, gu_cols, preferred_element_type=jnp.float32).astype(jnp.bfloat16)
    gu_act = gu_act.reshape(batch_loc, seq_len, n_tpb, 2, ff_block)
    mid_act = (jax.nn.silu(gu_act[..., 0, :].astype(jnp.float32)) * gu_act[..., 1, :].astype(jnp.float32)).astype(jnp.bfloat16)
    mid_act = mid_act.reshape(batch_loc, seq_len, n_tpb * ff_block)
    mlp_part = jnp.einsum('bsf,fd->bsd', mid_act, down_rows, preferred_element_type=jnp.float32).astype(jnp.bfloat16)
    mlp_sum = lax.psum(mlp_part, 'tpa')
    layer_out = (hidden.astype(jnp.float32) + mlp_sum.astype(jnp.float32)).astype(jnp.bfloat16)
    valid_pos = (positions[None, :] < len_loc[:, None])[:, :, None, None]
    k_cache = jnp.where(valid_pos, k_rot, k_buf)
    v_cache = jnp.where(valid_pos, values, v_buf)
    return layer_out, k_cache, v_cache


def solution(mesh):
    n_tpb = mesh.shape['tpb']

    def local_step(x_loc, len_loc, k_buf, v_buf, w_qkv, w_o, w_gate_up, w_down, g_attn, g_mlp):
        qkv_cols = lax.all_gather(w_qkv, 'tpb', axis=1, tiled=True)
        o_rows = lax.all_gather(w_o, 'tpb', axis=0, tiled=True)
        gu_cols = lax.all_gather(w_gate_up, 'tpb', axis=1, tiled=True)
        down_rows = lax.all_gather(w_down, 'tpb', axis=0, tiled=True)
        w_query, w_key, w_value, w_gate, w_up = split_weights(qkv_cols, gu_cols, k_buf.shape[2], k_buf.shape[3], n_tpb)
        layer_out, k_cache, v_cache = prefill(x_loc, len_loc, k_buf, v_buf, qkv_cols, o_rows, gu_cols, down_rows, g_attn, g_mlp, n_tpb)
        return (layer_out, k_cache, v_cache, w_query, w_key, w_value, o_rows, w_gate, w_up, down_rows)

    batch_spec = P(('part', 'tpb'), None, None)
    len_spec = P(('part', 'tpb'))
    cache_spec = P(('part', 'tpb'), None, 'tpa', None)
    train_cols = P('part', ('tpa', 'tpb'))
    train_rows = P(('part', 'tpa', 'tpb'), None)
    gain_spec = P('part')
    gen_cols = P('part', 'tpa')
    gen_rows = P(('part', 'tpa'), None)
    return jax.shard_map(local_step, mesh=mesh, in_specs=(batch_spec, len_spec, cache_spec, cache_spec, train_cols, train_rows, train_cols, train_rows, gain_spec, gain_spec), out_specs=(batch_spec, cache_spec, cache_spec, gen_cols, gen_cols, gen_cols, gen_rows, gen_cols, gen_cols, gen_rows), check_vma=False)
```

profile of v0, /device:TPU:97, one launch (start us, length us, event | category | flops | bytes accessed | tf_op | source)
XLA Modules:
  0.0 970.3 jit_solution(17599393141773063259)
XLA Ops:
  7.3 4.6 copy.34
  12.0 0.1 all-gather.7.cloned.1.call-start
  12.0 0.7 all-gather.7.cloned.1.call-update
  12.8 0.1 all-reduce.3.cloned.1.call-start
  12.9 5.1 fusion.2
  18.0 1.9 fusion.48
  20.6 1.3 fusion.31
  21.9 112.8 %all-gather.5.cloned.1.call-done = bf16[4096,3072]{0,1:T(8,128)(2,1)} async-done(((bf16[4096,384]{0,1:T(8,128)(2,1)}), bf16[4096,3072]{0,1:T(8,128)(2,1)}) %all-gather.5.cloned.1.call-update) | async-done | bytes 25165840 | tf_op jit(solution)/shard_map/all_gather | solution.py:95
  134.7 33.7 %fusion.26 = bf16[1024,3072]{1,0:T(8,128)(2,1)} fusion(bf16[4096,3072]{0,1:T(8,128)(2,1)} %all-gather.5.cloned.1.call-done, bf16[1,1024,4096]{2,1,0:T(8,128)(2,1)} %param.10, f32[4096]{0:T(1024)S(1)} %convert_element_type.123, f32[1024]{0:T(1024)S(1)} %add_rsqrt_fusion.1), kind=kOutput, calls=%fused_computation.38 | convolution fusion | flops 25789726720 | bytes 39866368 | tf_op jit(solution)/shard_map/bsd,dc->bsc/dot_general | solution.py:60
  168.4 8.6 copy.35
  177.0 5.7 fusion.58
  182.8 3.0 copy.54
  185.8 3.9 copy.55
  189.7 1.9 convert_element_type.128
  191.6 0.3 bitcast_convert_fusion
  191.9 1.5 subtract_convert_fusion.1
  193.4 3.5 fusion.32
  196.9 18.1 %fusion.1 = (f32[8,1024]{1,0:T(8,128)S(1)}, f32[8,1024,1024]{2,1,0:T(8,128)}) fusion(pred[1024,1024]{0,1:T(8,128)(4,1)S(1)} %copy-done.3, bf16[1024,8,64]{2,0,1:T(8,128)(2,1)} %get-tuple-element.41, bf16[1024,8,64]{2,0,1:T(8,128)(2,1)} %get-tuple-element.40, bf16[1024,8,64]{2,0,1:T(8,128)(2,1)S(1)} %bitcast.92, bf16[1024,8,64]{2,0,1:T(8,128)(2,1)S(1)} %bitcast.91), kind=kOutput, calls=%fused_computation.4 | convolution fusion | flops 2181029888 | bytes 38830080 | tf_op jit(solution)/shard_map/bqkgd,bskd->bkgqs/dot_general | solution.py:66
  214.9 14.2 %fusion = f32[8,1024]{1,0:T(8,128)S(1)} fusion(f32[8,1024,1024]{2,1,0:T(8,128)} %get-tuple-element.49, f32[8,1024]{1,0:T(8,128)S(1)} %get-tuple-element.48, pred[1024,1024]{0,1:T(8,128)(4,1)S(1)} %copy-done.3), kind=kLoop, calls=%fused_computation.3 | loop fusion | flops 33546240 | bytes 34668544 | tf_op jit(solution)/shard_map/reduce_sum | solution.py:70
  229.2 17.3 %fusion.42 = bf16[8,128,1024]{2,1,0:T(8,128)(2,1)} fusion(f32[8,1024]{1,0:T(8,128)S(1)} %fusion, f32[8,1024]{1,0:T(8,128)S(1)} %get-tuple-element.48, f32[8,1024,1024]{2,1,0:T(8,128)} %get-tuple-element.49, pred[1024,1024]{0,1:T(8,128)(4,1)S(1)} %copy-done.3, bf16[1,1024,8,3,128]{1,4,3,2,0:T(8,128)(2,1)} %bitcast.88), kind=kOutput, calls=%fused_computation.59 | convolution fusion | flops 2190475264 | bytes 38862848 | tf_op jit(solution)/shard_map/bkgqs,bskd->bqkgd/dot_general | solution.py:71
  246.4 15.1 %convert_bitcast_fusion.1 = bf16[1,1024,4096]{2,1,0:T(8,128)(2,1)} fusion(bf16[1024,1024]{0,1:T(8,128)(2,1)} %bitcast.95, bf16[1024,4096]{1,0:T(8,128)(2,1)} %all-gather.7.cloned.1.call-done), kind=kOutput, calls=%fused_computation.35 | convolution fusion | flops 8594128896 | bytes 18874368 | tf_op jit(solution)/shard_map/bsh,hd->bsd/dot_general | solution.py:73
  261.6 0.1 all-gather.9.cloned.1.call-start
  261.7 0.6 all-gather.9.cloned.1.call-update
  262.2 0.1 all-gather.11.cloned.1.call-start
  262.3 0.6 all-gather.11.cloned.1.call-update
  262.9 0.1 all-reduce.5.cloned.1.call-start
  263.0 153.9 %all-reduce.3.cloned.1.call-done = bf16[1,1024,4096]{2,1,0:T(8,128)(2,1)} async-done(((bf16[1,1024,4096]{2,1,0:T(8,128)(2,1)}), bf16[1,1024,4096]{2,1,0:T(8,128)(2,1)}) %all-reduce.3.cloned.1.call-update) | async-done | bytes 8388624 | tf_op jit(solution)/shard_map/psum | solution.py:74
  416.9 8.5 fusion.6
  425.5 197.2 %all-gather.9.cloned.1.call-done = bf16[4096,5504]{0,1:T(8,128)(2,1)} async-done(((bf16[4096,688]{0,1:T(8,128)(2,1)}), bf16[4096,5504]{0,1:T(8,128)(2,1)}) %all-gather.9.cloned.1.call-update) | async-done | bytes 45088784 | tf_op jit(solution)/shard_map/all_gather | solution.py:97
  622.6 58.1 %convolution_convert_fusion = bf16[1024,5504]{1,0:T(8,128)(2,1)} fusion(bf16[4096,5504]{0,1:T(8,128)(2,1)} %all-gather.9.cloned.1.call-done, f32[4096]{0:T(1024)S(1)} %convert_element_type.138, f32[1024]{0:T(1024)S(1)} %add_rsqrt_fusion, bf16[1,1024,4096]{2,1,0:T(8,128)(2,1)} %param.10, bf16[1,1024,4096]{2,1,0:T(8,128)(2,1)} %all-reduce.3.cloned.1.call-done), kind=kOutput, calls=%fused_computation.23 | convolution fusion | flops 46210088960 | bytes 73158656 | tf_op jit(solution)/shard_map/bsd,dc->bsc/dot_general | solution.py:78
  680.8 15.6 %copy.41 = bf16[1024,5504]{0,1:T(8,128)(2,1)} copy(bf16[1024,5504]{1,0:T(8,128)(2,1)} %convolution_convert_fusion) | data formatting | bytes 22544384 | tf_op jit(solution)/shard_map/convert_element_type | solution.py:78
  696.3 10.3 %fusion.57 = (bf16[1,1024,8,1,344]{1,4,3,2,0:T(8,128)(2,1)}, bf16[1,1024,8,1,344]{1,4,3,2,0:T(8,128)(2,1)}) fusion(bf16[1,1024,8,2,344]{1,4,3,2,0:T(8,128)(2,1)} %bitcast.82), kind=kLoop, calls=%fused_computation.75 | loop fusion | bytes 22544384 | tf_op jit(solution)/shard_map/slice | solution.py:80
  706.6 24.1 %all-gather.11.cloned.1.call-done = bf16[2752,4096]{1,0:T(8,128)(2,1)} async-done(((bf16[344,4096]{1,0:T(8,128)(2,1)}), bf16[2752,4096]{1,0:T(8,128)(2,1)}) %all-gather.11.cloned.1.call-update) | async-done | bytes 22544400 | tf_op jit(solution)/shard_map/all_gather | solution.py:98
  730.7 37.2 %convert_bitcast_fusion = bf16[1,1024,4096]{2,1,0:T(8,128)(2,1)} fusion(bf16[2752,4096]{1,0:T(8,128)(2,1)} %all-gather.11.cloned.1.call-done, bf16[1024,2752]{0,1:T(8,128)(2,1)} %bitcast.94, bf16[1024,2752]{0,1:T(8,128)(2,1)} %bitcast.93), kind=kOutput, calls=%fused_computation.32 | convolution fusion | flops 23112187904 | bytes 42205184 | tf_op jit(solution)/shard_map/bsf,fd->bsd/dot_general | solution.py:82
  768.0 1.5 copy-done
  769.5 2.4 copy.53
  771.9 5.1 bitcast_select_fusion.1
  777.0 2.7 copy.46
  779.6 2.7 copy.47
  782.3 16.8 %fusion.56 = (bf16[4096,8,1,128]{0,3,2,1:T(8,128)(2,1)}, bf16[4096,8,1,128]{0,3,2,1:T(8,128)(2,1)}, bf16[4096,8,1,128]{0,3,2,1:T(8,128)(2,1)}) fusion(bf16[4096,8,3,128]{0,3,2,1:T(8,128)(2,1)} %bitcast.86), kind=kLoop, calls=%fused_computation.74 | loop fusion | bytes 50331648 | tf_op jit(solution)/shard_map/slice | solution.py:46
  799.1 12.1 %copy.48 = bf16[4096,1024]{1,0:T(8,128)(2,1)} copy(bf16[4096,1024]{0,1:T(8,128)(2,1)} %bitcast.85) | data formatting | bytes 16777216
  811.2 11.9 %copy.49 = bf16[4096,1024]{1,0:T(8,128)(2,1)} copy(bf16[4096,1024]{0,1:T(8,128)(2,1)} %bitcast.84) | data formatting | bytes 16777216
  823.1 11.9 %copy.50 = bf16[4096,1024]{1,0:T(8,128)(2,1)} copy(bf16[4096,1024]{0,1:T(8,128)(2,1)} %bitcast.83) | data formatting | bytes 16777216
  835.1 29.8 %fusion.55 = (bf16[4096,8,1,344]{0,3,2,1:T(8,128)(2,1)}, bf16[4096,8,1,344]{0,3,2,1:T(8,128)(2,1)}) fusion(bf16[4096,8,2,344]{0,3,2,1:T(8,128)(2,1)} %bitcast.81), kind=kLoop, calls=%fused_computation.73 | loop fusion | bytes 90177536 | tf_op jit(solution)/shard_map/slice | solution.py:50
  864.9 58.3 %all-reduce.5.cloned.1.call-done = bf16[1,1024,4096]{2,1,0:T(8,128)(2,1)} async-done(((bf16[1,1024,4096]{2,1,0:T(8,128)(2,1)}), bf16[1,1024,4096]{2,1,0:T(8,128)(2,1)}) %all-reduce.5.cloned.1.call-update) | async-done | bytes 8388624 | tf_op jit(solution)/shard_map/psum | solution.py:83
  923.2 12.8 %fusion.9 = bf16[1,1024,4096]{2,1,0:T(8,128)(2,1)} fusion(bf16[1,1024,4096]{2,1,0:T(8,128)(2,1)} %all-reduce.5.cloned.1.call-done, bf16[1,1024,4096]{2,1,0:T(8,128)(2,1)} %all-reduce.3.cloned.1.call-done, bf16[1,1024,4096]{2,1,0:T(8,128)(2,1)} %param.10), kind=kLoop, calls=%fused_computation.18 | loop fusion | flops 33554432 | bytes 33554432 | tf_op jit(solution)/shard_map/convert_element_type | solution.py:84
  935.9 7.9 copy.65
  943.8 19.5 %copy.66 = bf16[2752,4096]{1,0:T(8,128)(2,1)} copy(bf16[2752,4096]{1,0:T(8,128)(2,1)} %all-gather.11.cloned.1.call-done) | data formatting | bytes 45088768
  (26 shorter events, 0.3 us)
Async XLA Ops:
  7.2 5.7 copy-start.4
  7.2 127.5 %all-gather.5.cloned.1.call-start = ((), (), s32[]{:S(2)}) async-start(), calls=%async_computation | async-start | bytes 28311552 | tf_op jit(solution)/shard_map/all_gather | solution.py:95
  12.0 234.5 %all-gather.7.cloned.1.call-start = ((), (), s32[]{:S(2)}) async-start(), calls=%async_computation.1 | async-start | bytes 9437184 | tf_op jit(solution)/shard_map/all_gather | solution.py:96
  12.8 404.1 %all-reduce.3.cloned.1.call-start = ((), (), s32[]{:S(2)}) async-start(), calls=%async_computation.2 | async-start | bytes 16777216 | tf_op jit(solution)/shard_map/psum | solution.py:74
  20.6 147.8 %copy-start.6 = (pred[1024]{0:T(1024)(128)(4,1)}, pred[1024]{0:T(1024)(128)(4,1)S(1)}, u32[]{:S(2)}) copy-start(pred[1024]{0:T(1024)(128)(4,1)S(1)} %iota_compare_fusion.1) | copy-start | bytes 3076
  193.3 21.6 %copy-start.1 = (bf16[1,1024,8,64]{3,1,2,0:T(8,128)(2,1)}, bf16[1,1024,8,64]{3,1,2,0:T(8,128)(2,1)S(1)}, u32[]{:S(2)}) copy-start(bf16[1,1024,8,64]{3,1,2,0:T(8,128)(2,1)S(1)} %get-tuple-element.42) | copy-start | bytes 3145732
  193.4 21.6 %copy-start.2 = (bf16[1,1024,8,64]{3,1,2,0:T(8,128)(2,1)}, bf16[1,1024,8,64]{3,1,2,0:T(8,128)(2,1)S(1)}, u32[]{:S(2)}) copy-start(bf16[1,1024,8,64]{3,1,2,0:T(8,128)(2,1)S(1)} %get-tuple-element.43) | copy-start | bytes 3145732
  193.4 3.5 copy-start.3
  261.5 1.4 copy-start.5
  261.6 361.1 %all-gather.9.cloned.1.call-start = ((), (), s32[]{:S(2)}) async-start(), calls=%async_computation.3 | async-start | bytes 50724864 | tf_op jit(solution)/shard_map/all_gather | solution.py:97
  262.2 468.4 %all-gather.11.cloned.1.call-start = ((), (), s32[]{:S(2)}) async-start(), calls=%async_computation.4 | async-start | bytes 25362432 | tf_op jit(solution)/shard_map/all_gather | solution.py:98
  262.9 660.3 %all-reduce.5.cloned.1.call-start = ((), (), s32[]{:S(2)}) async-start(), calls=%async_computation.5 | async-start | bytes 16777216 | tf_op jit(solution)/shard_map/psum | solution.py:83
  767.9 1.6 copy-start
  767.9 4.0 copy-start.7
Sparse Core Ops, SparseCore 0:
  12.1 122.5 all-gather.4
  136.3 47.8 all-gather.6
  261.7 155.1 all-reduce.2
  418.4 204.2 all-gather.8
  624.1 106.5 all-gather.10
  768.1 155.0 all-reduce.4
where the time goes:
time: 976 us; the launch traced here: 970 us
  waiting for transfers between devices  548 us (56%)
  matrix products  179 us (18%)
  local copies, waits for them, and re-layouts  171 us (18%)
  other arithmetic  56.1 us (6%)
  between operations  15.1 us (2%)
    all_gather x1, waiting for transfers between devices, local_step(): gu_cols = lax.all_gather(w_gate_up, 'tpb', axis=1, tiled=True)  197 us
    psum x1, waiting for transfers between devices, prefill(): attn_sum = lax.psum(attn_part, 'tpa')  154 us
    all_gather x1, waiting for transfers between devices, local_step(): qkv_cols = lax.all_gather(w_qkv, 'tpb', axis=1, tiled=True)  113 us
    unnamed x27, local copies, waits for them, and re-layouts  84.2 us
    psum x1, waiting for transfers between devices, prefill(): mlp_sum = lax.psum(mlp_part, 'tpa')  58.3 us
    dot_general x1, matrix products, prefill(): jnp.einsum('bsd,dc->bsc', h_normed, gu_cols, preferred_element_type=jnp.f...  58.1 us
    dot_general x1, matrix products, prefill(): jnp.einsum('bsf,fd->bsd', mid_act, down_rows, preferred_element_type=jnp....  37.2 us
    dot_general x1, matrix products, prefill(): jnp.einsum('bsd,dc->bsc', x_normed, qkv_cols, preferred_element_type=jnp....  33.7 us
  transfers between devices with their start and end apart: 6, of which 5 were waited for; matrix products, arithmetic and copies ran while one was open for 32% of the time, Pallas kernels for 0%

commit v1 on v0

v1 whole, which is shorter than its diff:
```python
import functools
import math

import jax
import jax.numpy as jnp
from jax import lax
from jax.experimental import pallas as pl
from jax.experimental.pallas import tpu as pltpu
from jax.sharding import PartitionSpec as P


ROPE_BASE = 500000.0
ROPE_FACTOR = 8.0
LOW_FREQ = 1.0
HIGH_FREQ = 4.0
ORIG_CONTEXT = 8192.0
NORM_EPS = 1e-5
MASK_VALUE = -1e30
MESH = pl.DeviceIdType.MESH
F32 = jnp.float32
BF16 = jnp.bfloat16


def rms_norm(x_in, gain_vec):
    x_wide = x_in.astype(F32)
    mean_sq = jnp.mean(x_wide * x_wide, axis=-1, keepdims=True)
    return (x_wide * lax.rsqrt(mean_sq + NORM_EPS) * gain_vec.astype(F32)).astype(BF16)


def rope_tables(seq_len, head_dim):
    exponent = jnp.arange(head_dim // 2, dtype=F32) * (2.0 / head_dim)
    inv_freq = 1.0 / jnp.power(ROPE_BASE, exponent)
    wavelen = 2.0 * math.pi / inv_freq
    smooth = (ORIG_CONTEXT / wavelen - LOW_FREQ) / (HIGH_FREQ - LOW_FREQ)
    blended = (1.0 - smooth) * inv_freq / ROPE_FACTOR + smooth * inv_freq
    rope_freq = jnp.where(wavelen < ORIG_CONTEXT / HIGH_FREQ, inv_freq, jnp.where(wavelen > ORIG_CONTEXT / LOW_FREQ, inv_freq / ROPE_FACTOR, blended))
    angles = jnp.arange(seq_len, dtype=F32)[:, None] * rope_freq[None, :]
    return jnp.cos(angles), jnp.sin(angles)


def qkv_kernel(u_ref, w_ref, cos_ref, sin_ref, q_ref, k_ref, v_ref, wq_ref, wk_ref, wv_ref):
    hd = cos_ref.shape[1]
    for i in range(2):
        cols = slice(i * hd, (i + 1) * hd)
        wq_ref[:, cols] = w_ref[i, :, 0:hd]
        wk_ref[:, cols] = w_ref[i, :, hd:2 * hd]
        wv_ref[:, cols] = w_ref[i, :, 2 * hd:3 * hd]
    rows = u_ref.shape[0] // 2

    def half(r, carry):
        sl = pl.ds(pl.multiple_of(r * rows, rows), rows)
        u = u_ref[sl, :]
        cos, sin = cos_ref[sl, :], sin_ref[sl, :]
        for src, dst in ((wq_ref, q_ref), (wk_ref, k_ref)):
            prod = jnp.dot(u, src[...], preferred_element_type=F32).astype(BF16).astype(F32)
            for i in range(2):
                p = prod[:, i * hd:(i + 1) * hd]
                dst[sl, i * hd:(i + 1) * hd] = (p * cos + pltpu.roll(p, hd // 2, 1) * sin).astype(BF16)
        v_ref[sl, :] = jnp.dot(u, wv_ref[...], preferred_element_type=F32).astype(BF16)
        return carry

    lax.fori_loop(0, 2, half, 0)


def qkv_call(u, wg, cos, sin):
    seq, dim = u.shape
    heads, _, packed = wg.shape
    hd = packed // 3
    wide = 2 * hd
    act = jax.ShapeDtypeStruct((seq, heads * hd), BF16)
    wout = jax.ShapeDtypeStruct((dim, heads * hd), BF16)
    act_spec = pl.BlockSpec((seq, wide), lambda h: (0, h))
    w_spec = pl.BlockSpec((dim, wide), lambda h: (0, h))
    one = pl.Buffered(1)
    return pl.pallas_call(
        qkv_kernel,
        grid=(heads // 2,),
        in_specs=[
            pl.BlockSpec((seq, dim), lambda h: (0, 0), pipeline_mode=one),
            pl.BlockSpec((2, dim, packed), lambda h: (h, 0, 0)),
            pl.BlockSpec((seq, hd), lambda h: (0, 0), pipeline_mode=one),
            pl.BlockSpec((seq, hd), lambda h: (0, 0), pipeline_mode=one),
        ],
        out_specs=[act_spec, act_spec, act_spec, w_spec, w_spec, w_spec],
        out_shape=[act, act, act, wout, wout, wout],
        compiler_params=pltpu.CompilerParams(vmem_limit_bytes=60 << 20),
        cost_estimate=pl.CostEstimate(flops=2 * seq * dim * heads * packed, bytes_accessed=4 * dim * heads * packed, transcendentals=0),
        name="qkv",
    )(u, wg, cos, sin)


def attn_kernel(scale, block, len_ref, q_ref, k_ref, v_ref, o_ref):
    seq = q_ref.shape[0]
    length = len_ref[0]
    for i in range(seq // block):
        lo, hi = i * block, (i + 1) * block
        s = lax.dot_general(q_ref[lo:hi, :], k_ref[0:hi, :], (((1,), (1,)), ((), ())), preferred_element_type=F32) * scale
        row = lo + lax.broadcasted_iota(jnp.int32, s.shape, 0)
        col = lax.broadcasted_iota(jnp.int32, s.shape, 1)
        s = jnp.where((col <= row) & (col < length), s, MASK_VALUE)
        e = jnp.exp(s - jnp.max(s, axis=-1, keepdims=True))
        w = (e * (1.0 / jnp.sum(e, axis=-1, keepdims=True))).astype(BF16)
        o_ref[lo:hi, :] = jnp.dot(w, v_ref[0:hi, :], preferred_element_type=F32).astype(BF16)


def attn_call(length, q, k, v, hd):
    seq, width = q.shape
    heads = width // hd
    spec = pl.BlockSpec((seq, hd), lambda h: (0, h))
    return pl.pallas_call(
        functools.partial(attn_kernel, hd ** -0.5, 256),
        grid=(heads,),
        in_specs=[pl.BlockSpec(memory_space=pltpu.SMEM), spec, spec, spec],
        out_specs=spec,
        out_shape=jax.ShapeDtypeStruct((seq, width), BF16),
        compiler_params=pltpu.CompilerParams(vmem_limit_bytes=48 << 20),
        cost_estimate=pl.CostEstimate(flops=4 * seq * seq * width, bytes_accessed=8 * seq * width, transcendentals=seq * seq * heads),
        name="attn",
    )(length, q, k, v)


def gate_up_kernel(u_ref, w_ref, m_ref, wg_ref, wu_ref):
    ff = wg_ref.shape[1]
    wg_ref[0] = w_ref[0, 0:ff, :]
    wu_ref[0] = w_ref[0, ff:2 * ff, :]
    seq = u_ref.shape[0]
    tile = 256

    def part(j, carry):
        sl = pl.ds(pl.multiple_of(j * tile, tile), tile)
        both = lax.dot_general(w_ref[0], u_ref[sl, :], (((1,), (1,)), ((), ())), preferred_element_type=F32)
        gate = both[0:ff].astype(BF16).astype(F32)
        up = both[ff:2 * ff].astype(BF16).astype(F32)
        m_ref[0, :, sl] = (gate * jax.nn.sigmoid(gate) * up).astype(BF16)
        return carry

    lax.fori_loop(0, seq // tile, part, 0)


def gate_up_call(u, wg):
    seq, dim = u.shape
    blocks, rows, _ = wg.shape
    ff = rows // 2
    wout = jax.ShapeDtypeStruct((blocks, ff, dim), BF16)
    wspec = pl.BlockSpec((1, ff, dim), lambda h: (h, 0, 0))
    return pl.pallas_call(
        gate_up_kernel,
        grid=(blocks,),
        in_specs=[
            pl.BlockSpec((seq, dim), lambda h: (0, 0), pipeline_mode=pl.Buffered(1)),
            pl.BlockSpec((1, rows, dim), lambda h: (h, 0, 0)),
        ],
        out_specs=[pl.BlockSpec((1, ff, seq), lambda h: (h, 0, 0)), wspec, wspec],
        out_shape=[jax.ShapeDtypeStruct((blocks, ff, seq), BF16), wout, wout],
        compiler_params=pltpu.CompilerParams(vmem_limit_bytes=60 << 20),
        cost_estimate=pl.CostEstimate(flops=2 * seq * dim * blocks * rows, bytes_accessed=4 * dim * blocks * rows, transcendentals=seq * ff * blocks),
        name="gate_up",
    )(u, wg)


CHUNKS = 2
COPIES = 12


def sum_kernel(n, transposed, col0, a_ref, w_ref, res_ref, out_ref, a_buf, w_buf, res_buf, part, own, first, second, gath, in_sem, out_sem, send_sem, recv_sem):
    me = lax.axis_index("tpa")
    right, left, far = lax.rem(me + 1, n), lax.rem(me + n - 1, n), lax.rem(me + 2, n)
    order = (far, right, left, me)
    shard, width = own.shape
    half = width // 2
    rows = shard // CHUNKS
    tile = w_buf.shape[2]
    tiles = w_buf.shape[0]

    loads = []
    for s in range(n):
        span = pl.ds(pl.multiple_of(order[s] * shard, shard), shard)
        src = a_ref.at[:, span] if transposed else a_ref.at[span, :]
        loads.append(pltpu.make_async_copy(src, a_buf.at[s], in_sem.at[s]))
    wloads = [pltpu.make_async_copy(w_ref.at[:, t * tile:(t + 1) * tile], w_buf.at[t], in_sem.at[n + t]) for t in range(tiles)]
    mine = pl.ds(pl.multiple_of(me * shard, shard), shard)
    res_load = pltpu.make_async_copy(res_ref.at[mine, col0:col0 + width], res_buf, in_sem.at[n + tiles])
    loads[0].start()
    for c in wloads:
        c.start()
    for c in loads[1:]:
        c.start()
    res_load.start()

    barrier = pltpu.get_barrier_semaphore()
    for peer in (left, right):
        pl.semaphore_signal(barrier, inc=1, device_id={"tpa": peer}, device_id_type=MESH)
    pl.semaphore_wait(barrier, 2)

    A, B = slice(0, half), slice(half, width)

    def span_of(c):
        return slice(c * rows, (c + 1) * rows)

    def send(c, i, src, dst, peer):
        cp = pltpu.make_async_remote_copy(src_ref=src, dst_ref=dst, send_sem=send_sem.at[c, i], recv_sem=recv_sem.at[c, i], device_id={"tpa": peer}, device_id_type=MESH)
        cp.start()
        return cp

    dims = (((0,), (0,)), ((), ())) if transposed else (((1,), (0,)), ((), ()))

    def product(s, t):
        return lax.dot_general(a_buf[s], w_buf[t], dims, preferred_element_type=F32)

    sent = {}
    loads[0].wait()
    for t in range(tiles):
        wloads[t].wait()
        part[0, :, t * tile:(t + 1) * tile] = product(0, t).astype(BF16)
    for c in range(CHUNKS):
        r = span_of(c)
        sent[c, 0] = send(c, 0, part.at[0, r, A], first.at[0, r, :], right)
        sent[c, 1] = send(c, 1, part.at[0, r, B], first.at[1, r, :], left)
    for s in (1, 2):
        loads[s].wait()
        for t in range(tiles):
            part[s, :, t * tile:(t + 1) * tile] = product(s, t).astype(BF16)
        for c in range(CHUNKS):
            r = span_of(c)
            if s == 1:
                sent[c, 2] = send(c, 2, part.at[1, r, B], second.at[0, r, B], right)
            else:
                sent[c, 3] = send(c, 3, part.at[2, r, A], second.at[1, r, A], left)
    loads[3].wait()
    res_load.wait()
    for t in range(tiles):
        cols = slice(t * tile, (t + 1) * tile)
        own[:, cols] = res_buf[:, cols].astype(F32) + product(3, t)

    for c in range(CHUNKS):
        r = span_of(c)
        sent[c, 0].wait_recv()
        part[1, r, A] = (part[1, r, A].astype(F32) + first[0, r, :].astype(F32)).astype(BF16)
        sent[c, 4] = send(c, 4, part.at[1, r, A], second.at[0, r, A], right)
        sent[c, 1].wait_recv()
        part[2, r, B] = (part[2, r, B].astype(F32) + first[1, r, :].astype(F32)).astype(BF16)
        sent[c, 5] = send(c, 5, part.at[2, r, B], second.at[1, r, B], left)

    stores = []

    def store(c, slot, owner, i, cols):
        r = span_of(c)
        dst = out_ref.at[pl.ds(pl.multiple_of(owner * shard + c * rows, rows), rows), cols]
        cp = pltpu.make_async_copy(gath.at[slot, r, cols], dst, out_sem.at[c, i])
        cp.start()
        stores.append(cp)

    for c in range(CHUNKS):
        r = span_of(c)
        for i in (2, 4, 3, 5):
            sent[c, i].wait_recv()
        total = own[r, :] + second[0, r, :].astype(F32) + second[1, r, :].astype(F32)
        gath[0, r, :] = total.astype(BF16)
        sent[c, 6] = send(c, 6, gath.at[0, r, A], gath.at[1, r, A], right)
        sent[c, 7] = send(c, 7, gath.at[0, r, B], gath.at[2, r, B], left)
        sent[c, 8] = send(c, 8, gath.at[0, r, B], gath.at[1, r, B], right)
        sent[c, 9] = send(c, 9, gath.at[0, r, A], gath.at[2, r, A], left)
        store(c, 0, me, 0, slice(0, width))
    for c in range(CHUNKS):
        r = span_of(c)
        sent[c, 6].wait_recv()
        sent[c, 10] = send(c, 10, gath.at[1, r, A], gath.at[3, r, A], right)
        sent[c, 7].wait_recv()
        sent[c, 11] = send(c, 11, gath.at[2, r, B], gath.at[3, r, B], left)
        store(c, 1, left, 1, A)
        store(c, 2, right, 2, B)
    for c in range(CHUNKS):
        sent[c, 8].wait_recv()
        store(c, 1, left, 3, B)
        sent[c, 9].wait_recv()
        store(c, 2, right, 4, A)
    for c in range(CHUNKS):
        sent[c, 10].wait_recv()
        store(c, 3, far, 5, A)
        sent[c, 11].wait_recv()
        store(c, 3, far, 6, B)
    for cp in sent.values():
        cp.wait_send()
    for cp in stores:
        cp.wait()


def sum_call(n, a, w, res, col0, cid, transposed):
    depth, width = w.shape
    seq = res.shape[0]
    shard = seq // n
    tile = 512
    tiles = width // tile
    any_spec = pl.BlockSpec(memory_space=pl.ANY)
    a_shape = (n, depth, shard) if transposed else (n, shard, depth)
    return pl.pallas_call(
        functools.partial(sum_kernel, n, transposed, col0),
        in_specs=[any_spec] * 3,
        out_specs=any_spec,
        out_shape=jax.ShapeDtypeStruct((seq, width), BF16),
        scratch_shapes=[
            pltpu.VMEM(a_shape, BF16),
            pltpu.VMEM((tiles, depth, tile), BF16),
            pltpu.VMEM((shard, width), BF16),
            pltpu.VMEM((3, shard, width), BF16),
            pltpu.VMEM((shard, width), F32),
            pltpu.VMEM((2, shard, width // 2), BF16),
            pltpu.VMEM((2, shard, width), BF16),
            pltpu.VMEM((4, shard, width), BF16),
            pltpu.SemaphoreType.DMA((n + tiles + 1,)),
            pltpu.SemaphoreType.DMA((CHUNKS, 7)),
            pltpu.SemaphoreType.DMA((CHUNKS, COPIES)),
            pltpu.SemaphoreType.DMA((CHUNKS, COPIES)),
        ],
        compiler_params=pltpu.CompilerParams(collective_id=cid, has_side_effects=True, vmem_limit_bytes=62 << 20),
        cost_estimate=pl.CostEstimate(flops=2 * seq * depth * width + 130_000_000_000, bytes_accessed=2 * depth * width, transcendentals=0),
    )(a, w, res)


def copy_kernel(src_ref, dst_ref):
    dst_ref[...] = src_ref[...]


def copy_call(w):
    rows, width = w.shape
    block = rows // 8
    spec = pl.BlockSpec((block, width), lambda i: (i, 0))
    return pl.pallas_call(
        copy_kernel,
        grid=(rows // block,),
        in_specs=[spec],
        out_specs=spec,
        out_shape=jax.ShapeDtypeStruct((rows, width), w.dtype),
        compiler_params=pltpu.CompilerParams(vmem_limit_bytes=32 << 20),
        cost_estimate=pl.CostEstimate(flops=rows * width, bytes_accessed=4 * rows * width, transcendentals=0),
    )(w)


def solution(mesh):
    n_tpa = mesh.shape['tpa']
    assert n_tpa == 4

    def gather(w, tiled):
        return lax.all_gather(w, 'tpb', axis=0, tiled=tiled)

    def layer(x_loc, len_loc, k_buf, v_buf, w_qkv, w_o, w_gate_up, w_down, g_attn, g_mlp):
        seq, dim = x_loc.shape[1:]
        heads, hd = k_buf.shape[2:]
        half = dim // 2
        x = x_loc[0]
        qkv_g = gather(w_qkv, False)
        o_g = gather(w_o, True)
        gu_g = gather(w_gate_up.T, False)
        down_a = gather(w_down[:, :half], True)
        down_b = gather(w_down[:, half:], True)

        cos, sin = rope_tables(seq, hd)
        cos2 = jnp.concatenate([cos, cos], axis=-1)
        sin2 = jnp.concatenate([-sin, sin], axis=-1)
        u = rms_norm(x, g_attn)
        q, k, v, w_q, w_k, w_v = qkv_call(u, qkv_g, cos2, sin2)
        att = attn_call(len_loc, q, k, v, hd)
        hidden = sum_call(n_tpa, att, o_g, x, 0, 0, False)

        valid = (jnp.arange(seq) < len_loc[0])[:, None, None]
        k_cache = jnp.where(valid, k.reshape(seq, heads, hd), k_buf[0])[None]
        v_cache = jnp.where(valid, v.reshape(seq, heads, hd), v_buf[0])[None]
        o_out = copy_call(o_g)

        u2 = rms_norm(hidden, g_mlp)
        u2, k_cache, v_cache, o_out = lax.optimization_barrier((u2, k_cache, v_cache, o_out))
        m_t, gate_t, up_t = gate_up_call(u2, gu_g)
        ff = m_t.shape[0] * m_t.shape[1]
        m_t = m_t.reshape(ff, seq)
        y_a = sum_call(n_tpa, m_t, down_a, hidden, 0, 1, True)
        y_b = sum_call(n_tpa, m_t, down_b, hidden, half, 2, True)
        y = jnp.concatenate([y_a, y_b], axis=1)[None]
        down_a, down_b, _ = lax.optimization_barrier((down_a, down_b, y_a))
        down = jnp.concatenate([down_a, down_b], axis=1)
        return (y, k_cache, v_cache, w_q, w_k, w_v, o_out, gate_t.reshape(ff, dim).T, up_t.reshape(ff, dim).T, down)

    batch_spec = P(('part', 'tpb'), None, None)
    len_spec = P(('part', 'tpb'))
    cache_spec = P(('part', 'tpb'), None, 'tpa', None)
    train_cols = P('part', ('tpa', 'tpb'))
    train_rows = P(('part', 'tpa', 'tpb'), None)
    gain_spec = P('part')
    gen_cols = P('part', 'tpa')
    gen_rows = P(('part', 'tpa'), None)
    return jax.shard_map(layer, mesh=mesh, in_specs=(batch_spec, len_spec, cache_spec, cache_spec, train_cols, train_rows, train_cols, train_rows, gain_spec, gain_spec), out_specs=(batch_spec, cache_spec, cache_spec, gen_cols, gen_cols, gen_cols, gen_rows, gen_cols, gen_cols, gen_rows), check_vma=False)
```

time: 976 us -> 671 us (0.69)
  Pallas kernels: 0 us -> 426 us
  waiting for transfers between devices: 548 us -> 142 us
  matrix products: 179 us -> 0 us
  local copies, waits for them, and re-layouts: 171 us -> 9.46 us
  other arithmetic: 56.1 us -> 70.3 us
    pallas_call x0 -> x7, Pallas kernels: none -> 426 us  [the longest x3 297 us: sum_call(): pl.pallas_call(functools.partial(sum_kernel, n, transposed, col0), in_spe...]
    psum x2 -> x0, waiting for transfers between devices: 212 us -> none  [the longest x1 154 us: prefill(): attn_sum = lax.psum(attn_part, 'tpa')]
    all_gather x4 -> x5, waiting for transfers between devices: 334 us -> 139 us  [gather(): return lax.all_gather(w, 'tpb', axis=0, tiled=tiled)]
    dot_general x6 -> x0, matrix products: 179 us -> none  [the longest x1 58.1 us: prefill(): jnp.einsum('bsd,dc->bsc', h_normed, gu_cols, preferred_element_type=jnp.f...]
    unnamed x27 -> x26, local copies, waits for them, and re-layouts: 84.2 us -> 7.74 us
    slice x4 -> x1, local copies, waits for them, and re-layouts: 62.6 us -> 1.72 us  [layer(): down_a = gather(w_down[:, :half], True)]
    convert_element_type x2 -> x0, local copies, waits for them, and re-layouts: 24.2 us -> none  [the longest x1 15.6 us: prefill(): jnp.einsum('bsd,dc->bsc', h_normed, gu_cols, preferred_element_type=jnp.f...]
    concatenate x1 -> x2, other arithmetic: 3.48 us -> 21.3 us  [the longest x1 20 us: layer(): down = jnp.concatenate([down_a, down_b], axis=1)]
  transfers between devices with their start and end apart: 6 -> 5, of which waited for: 5 -> 2; matrix products, arithmetic and copies ran while one was open for 32% -> 7% of each run, Pallas kernels for 0% -> 53%
where the time goes in v1:
time: 671 us; the launch traced here: 663 us
  Pallas kernels  426 us (63%)
  waiting for transfers between devices  142 us (21%)
  other arithmetic  70.3 us (10%)
  between operations  14.9 us (2%)
  local copies, waits for them, and re-layouts  9.46 us (1%)
    pallas_call x3, Pallas kernels, sum_call(): pl.pallas_call(functools.partial(sum_kernel, n, transposed, col0), in_spe...  297 us
    all_gather x5, waiting for transfers between devices, gather(): return lax.all_gather(w, 'tpb', axis=0, tiled=tiled)  139 us
    pallas_call x1, Pallas kernels, gate_up_call(): pl.pallas_call(gate_up_kernel, grid=(blocks,), in_specs=[pl.BlockSpec((se...  64.2 us
    pallas_call x1, Pallas kernels, qkv_call(): pl.pallas_call(qkv_kernel, grid=(heads // 2,), in_specs=[pl.BlockSpec((se...  40.9 us
    convert_element_type x2, other arithmetic, rms_norm(): (x_wide * lax.rsqrt(mean_sq + NORM_EPS) * gain_vec.astype(F32)).astype(BF16)  22.1 us
    pallas_call x1, Pallas kernels, attn_call(): pl.pallas_call(functools.partial(attn_kernel, hd ** (-0.5), 256), grid=(h...  20 us
    concatenate x1, other arithmetic, layer(): down = jnp.concatenate([down_a, down_b], axis=1)  20 us
  transfers between devices with their start and end apart: 5, of which 2 were waited for; matrix products, arithmetic and copies ran while one was open for 7% of the time, Pallas kernels for 53%

profile of v1, /device:TPU:97, one launch (start us, length us, event | category | flops | bytes accessed | tf_op | source)
XLA Modules:
  0.0 663.0 jit_solution(11137835435338204227)
XLA Ops:
  7.2 0.0 copy-start.3
  7.2 0.1 all-gather.8.cloned.1.call-start
  7.3 0.7 all-gather.8.cloned.1.call-update
  8.0 0.1 all-gather.14.cloned.1.call-start
  8.1 0.7 all-gather.14.cloned.1.call-update
  8.8 0.0 copy-start.9
  8.8 0.1 all-gather.16.cloned.1.call-start
  8.9 0.7 all-gather.16.cloned.1.call-update
  9.6 0.0 copy-start.10
  9.6 0.1 all-gather.10.cloned.1.call-start
  9.7 1.7 fusion.9
  11.4 0.1 all-gather.10.cloned.1.call-update
  11.5 0.1 all-gather.12.cloned.1.call-start
  11.6 0.6 all-gather.12.cloned.1.call-update
  12.2 2.0 fusion.8
  14.1 5.1 fusion
  19.9 0.6 convert_element_type.22
  20.5 0.6 iota_compare_fusion
  21.1 11.4 %fusion.2.u_ref = bf16[1024,4096]{1,0:T(8,128)(2,1)} fusion(f32[4096]{0:T(1024)S(1)} %convert_element_type.19, f32[1024]{0:T(1024)S(1)} %add_rsqrt_fusion.1, bf16[1,1024,4096]{2,1,0:T(8,128)(2,1)} %param.10), kind=kLoop, calls=%fused_computation.7 | loop fusion | flops 16777216 | bytes 16797696 | tf_op jit(solution)/shard_map/convert_element_type | solution.py:27
  32.5 1.3 pad_maximum_fusion.1
  33.8 27.3 %all-gather.8.cloned.1.call-done.w_ref.src_ref = bf16[1024,4096]{1,0:T(8,128)(2,1)} async-done(((bf16[128,4096]{1,0:T(8,128)(2,1)}), bf16[1024,4096]{1,0:T(8,128)(2,1)}) %all-gather.8.cloned.1.call-update) | async-done | bytes 8388624 | tf_op jit(solution)/shard_map/all_gather | solution.py:344
  61.1 3.4 copy-done
  64.5 4.7 shard_map.178
  69.2 111.4 %all-gather.14.cloned.1.call-done = bf16[32768,384]{1,0:T(8,128)(2,1)} async-done(((bf16[4096,384]{1,0:T(8,128)(2,1)}), bf16[32768,384]{1,0:T(8,128)(2,1)}) %all-gather.14.cloned.1.call-update) | async-done | bytes 25165840 | tf_op jit(solution)/shard_map/all_gather | solution.py:344
  180.6 40.9 %qkv.1 = (bf16[1024,1024]{1,0:T(8,128)(2,1)}, bf16[1024,1024]{1,0:T(8,128)(2,1)}, bf16[1024,1024]{1,0:T(8,128)(2,1)}, bf16[4096,1024]{1,0:T(8,128)(2,1)}, bf16[4...) custom-call(bf16[1024,4096]{1,0:T(8,128)(2,1)} %fusion.2.u_ref, bf16[8,4096,384]{2,1,0:T(8,128)(2,1)} %bitcast.33, ...), custom_call_target="tpu_custom_call" | custom-call | flops 25769803776 | bytes 50331648 | tf_op jit(solution)/shard_map/qkv/pallas_call | solution.py:75
  221.5 1.6 copy-done.1
  223.1 20.0 %attn.1.a_ref = bf16[1024,1024]{1,0:T(8,128)(2,1)S(1)} custom-call(s32[1]{0:T(128)} %copy.22.len_ref, bf16[1024,1024]{1,0:T(8,128)(2,1)S(1)} %copy-done.1, bf16[1024,1024]{1,0:T(8,128)(2,1)} %get-tuple-element.26.k_ref, bf16[1024,1024]{1,0:T(8,128)(2,1)} %get-tuple-element.27.v_ref), custom_call_target="tpu_custom_call" | custom-call | flops 4294967296 | bytes 8388608 | tf_op jit(solution)/shard_map/attn/pallas_call | solution.py:110
  243.2 0.0 copy-start.2
  243.2 1.3 copy-done.2
  244.5 144.7 %shard_map.177.res_ref = bf16[1024,4096]{1,0:T(8,128)(2,1)} custom-call(bf16[1024,1024]{1,0:T(8,128)(2,1)} %copy-done.2, bf16[1024,4096]{1,0:T(8,128)(2,1)} %all-gather.8.cloned.1.call-done.w_ref.src_ref, bf16[1024,4096]{1,0:T(8,128)(2,1)} %bitcast.26), custom_call_target="tpu_custom_call" | custom-call | flops 138589929472 | bytes 8388608 | tf_op jit(solution)/shard_map/pallas_call | solution.py:296
  389.2 0.0 copy-start.7
  389.2 0.0 copy-start.6
  389.2 0.0 copy-start.4
  389.2 0.0 copy-start.5
  389.2 5.2 fusion.3
  394.5 0.6 copy.20
  395.1 0.6 copy.21
  395.8 0.0 copy-done.4
  395.8 0.1 copy-done.5
  395.9 5.5 bitcast_select_fusion
  401.4 0.0 copy-done.8
  401.4 10.7 %fusion.5.u_ref = bf16[1024,4096]{1,0:T(8,128)(2,1)} fusion(bf16[1024,4096]{1,0:T(8,128)(2,1)} %shard_map.177.res_ref, f32[4096]{0:T(1024)S(1)} %copy-done.8, f32[1024]{0:T(1024)S(1)} %add_rsqrt_fusion), kind=kLoop, calls=%fused_computation.10 | loop fusion | flops 16777216 | bytes 16797696 | tf_op jit(solution)/shard_map/convert_element_type | solution.py:27
  412.1 64.2 %gate_up.1 = (bf16[8,344,1024]{2,1,0:T(8,128)(2,1)}, bf16[8,344,4096]{2,1,0:T(8,128)(2,1)}, bf16[8,344,4096]{2,1,0:T(8,128)(2,1)}) custom-call(bf16[1024,4096]{1,0:T(8,128)(2,1)} %fusion.5.u_ref, bf16[8,688,4096]{2,1,0:T(8,128)(2,1)} %bitcast.32), custom_call_target="tpu_custom_call" | custom-call | flops 46170898432 | bytes 90177536 | tf_op jit(solution)/shard_map/gate_up/pallas_call | solution.py:146
  476.3 75.7 %shard_map.179 = bf16[1024,2048]{1,0:T(8,128)(2,1)} custom-call(bf16[2752,1024]{1,0:T(8,128)(2,1)} %bitcast.36, bf16[2752,2048]{1,0:T(8,128)(2,1)} %all-gather.10.cloned.1.call-done.w_ref, bf16[1024,4096]{1,0:T(8,128)(2,1)} %shard_map.177.res_ref), custom_call_target="tpu_custom_call" | custom-call | flops 141542719488 | bytes 11272192 | tf_op jit(solution)/shard_map/pallas_call | solution.py:296
  552.0 0.0 all-gather.12.cloned.1.call-done.w_ref
  552.0 76.3 %shard_map.180 = bf16[1024,2048]{1,0:T(8,128)(2,1)} custom-call(bf16[2752,1024]{1,0:T(8,128)(2,1)} %bitcast.37, bf16[2752,2048]{1,0:T(8,128)(2,1)} %all-gather.12.cloned.1.call-done.w_ref, bf16[1024,4096]{1,0:T(8,128)(2,1)} %shard_map.177.res_ref), custom_call_target="tpu_custom_call" | custom-call | flops 141542719488 | bytes 11272192 | tf_op jit(solution)/shard_map/pallas_call | solution.py:296
  628.4 8.0 %maximum_bitcast_fusion = bf16[1,1024,4096]{2,1,0:T(8,128)(2,1)} fusion(bf16[1024,2048]{1,0:T(8,128)(2,1)} %shard_map.180, bf16[1024,2048]{1,0:T(8,128)(2,1)} %shard_map.179), kind=kLoop, calls=%fused_computation.11 | loop fusion | flops 16777216 | bytes 16777216 | tf_op jit(solution)/shard_map/broadcast_in_dim | solution.py:377
  636.3 20.0 %pad_maximum_fusion = bf16[2752,4096]{1,0:T(8,128)(2,1)} fusion(bf16[2752,2048]{1,0:T(8,128)(2,1)} %all-gather.12.cloned.1.call-done.w_ref, bf16[2752,2048]{1,0:T(8,128)(2,1)} %all-gather.10.cloned.1.call-done.w_ref), kind=kLoop, calls=%fused_computation | loop fusion | flops 45088768 | bytes 45088768 | tf_op jit(solution)/shard_map/concatenate | solution.py:379
  (16 shorter events, 0.1 us)
Async XLA Ops:
  7.2 2.5 copy-start.3
  7.2 53.9 %all-gather.8.cloned.1.call-start = ((), (), s32[]{:S(2)}) async-start(), calls=%async_computation | async-start | bytes 9437184 | tf_op jit(solution)/shard_map/all_gather | solution.py:344
  8.0 172.6 %all-gather.14.cloned.1.call-start = ((), (), s32[]{:S(2)}) async-start(), calls=%async_computation.3 | async-start | bytes 28311552 | tf_op jit(solution)/shard_map/all_gather | solution.py:344
  8.8 5.3 copy-start.9
  8.8 403.3 %all-gather.16.cloned.1.call-start = ((), (), s32[]{:S(2)}) async-start(), calls=%async_computation.4 | async-start | bytes 50724864 | tf_op jit(solution)/shard_map/all_gather | solution.py:344
  9.6 10.3 %copy-start.10 = (bf16[4096]{0:T(1024)(128)(2,1)S(1)}, bf16[4096]{0:T(1024)(128)(2,1)}, u32[]{:S(2)}) copy-start(bf16[4096]{0:T(1024)(128)(2,1)} %param.19) | copy-start | bytes 24580
  9.6 466.7 %all-gather.10.cloned.1.call-start = ((), (), s32[]{:S(2)}) async-start(), calls=%async_computation.1 | async-start | bytes 12681216 | tf_op jit(solution)/shard_map/all_gather | solution.py:344
  11.5 540.5 %all-gather.12.cloned.1.call-start = ((), (), s32[]{:S(2)}) async-start(), calls=%async_computation.2 | async-start | bytes 12681216 | tf_op jit(solution)/shard_map/all_gather | solution.py:344
  61.1 3.4 copy-start
  221.5 1.6 copy-start.1
  243.2 1.3 copy-start.2
  389.2 5.3 copy-start.7
  389.2 5.9 copy-start.6
  389.2 6.6 copy-start.4
  389.2 6.7 %copy-start.5 = (bf16[1,1024,8,128]{3,2,1,0:T(8,128)(2,1)S(1)}, bf16[1,1024,8,128]{3,2,1,0:T(8,128)(2,1)}, u32[]{:S(2)}) copy-start(bf16[1,1024,8,128]{3,2,1,0:T(8,128)(2,1)} %param.12) | copy-start | bytes 6291460
  389.2 6.7 %copy-start.11 = (pred[1024]{0:T(1024)(128)(4,1)S(1)}, pred[1024]{0:T(1024)(128)(4,1)}, u32[]{:S(2)}) copy-start(pred[1024]{0:T(1024)(128)(4,1)} %iota_compare_fusion) | copy-start | bytes 3076
  395.1 6.3 copy-start.8
Sparse Core Ops, SparseCore 0:
  9.7 51.4 all-gather.7
  62.7 117.8 all-gather.13
  182.2 203.8 all-gather.15
  387.5 58.6 all-gather.9
  447.7 59.5 all-gather.11

commit v2 on v1

v2 whole, which is shorter than its diff:
```python
import functools
import math

import jax
import jax.numpy as jnp
from jax import lax
from jax.experimental import pallas as pl
from jax.experimental.pallas import tpu as pltpu
from jax.sharding import PartitionSpec as P


ROPE_BASE = 500000.0
ROPE_FACTOR = 8.0
LOW_FREQ = 1.0
HIGH_FREQ = 4.0
ORIG_CONTEXT = 8192.0
NORM_EPS = 1e-5
MASK_VALUE = -1e30
MESH = pl.DeviceIdType.MESH
F32 = jnp.float32
BF16 = jnp.bfloat16


def rope_tables(seq_len, head_dim):
    exponent = jnp.arange(head_dim // 2, dtype=F32) * (2.0 / head_dim)
    inv_freq = 1.0 / jnp.power(ROPE_BASE, exponent)
    wavelen = 2.0 * math.pi / inv_freq
    smooth = (ORIG_CONTEXT / wavelen - LOW_FREQ) / (HIGH_FREQ - LOW_FREQ)
    blended = (1.0 - smooth) * inv_freq / ROPE_FACTOR + smooth * inv_freq
    rope_freq = jnp.where(wavelen < ORIG_CONTEXT / HIGH_FREQ, inv_freq, jnp.where(wavelen > ORIG_CONTEXT / LOW_FREQ, inv_freq / ROPE_FACTOR, blended))
    angles = jnp.arange(seq_len, dtype=F32)[:, None] * rope_freq[None, :]
    return jnp.cos(angles), jnp.sin(angles)


PIECES = 4


def gather_qkv_kernel(chips, x_ref, gain_ref, w_ref, cos_ref, sin_ref, q_ref, k_ref, v_ref, all_ref, u_buf, w_buf, gain_buf, cos_buf, sin_buf, acc, in_sem, out_sem, send_sem, recv_sem):
    here = lax.axis_index("tpb")
    chip, core = here // 2, lax.rem(here, 2)
    right, left, far = lax.rem(chip + 1, chips), lax.rem(chip + chips - 1, chips), lax.rem(chip + 2, chips)
    other = 1 - core
    mate = 2 * chip + other
    dim, packed = w_ref.shape
    hd = packed // 3
    seq = x_ref.shape[0]
    depth = dim // PIECES
    mid = dim // 2
    A, B = slice(0, mid), slice(mid, dim)

    loads = [
        pltpu.make_async_copy(w_ref, w_buf.at[here], in_sem.at[0]),
        pltpu.make_async_copy(x_ref, u_buf, in_sem.at[1]),
        pltpu.make_async_copy(cos_ref, cos_buf, in_sem.at[2]),
        pltpu.make_async_copy(sin_ref, sin_buf, in_sem.at[3]),
        pltpu.make_async_copy(gain_ref, gain_buf, in_sem.at[4]),
    ]
    barrier = pltpu.get_barrier_semaphore()
    for peer in (2 * left + core, 2 * right + core, mate):
        pl.semaphore_signal(barrier, inc=1, device_id={"tpb": peer}, device_id_type=MESH)
    pl.semaphore_wait(barrier, 3)

    def send(i, src, slot, rows, peer):
        cp = pltpu.make_async_remote_copy(src_ref=src, dst_ref=w_buf.at[slot, rows, :], send_sem=send_sem.at[i], recv_sem=recv_sem.at[i], device_id={"tpb": peer}, device_id_type=MESH)
        cp.start()
        return cp

    def piece(j):
        return slice(j * depth, (j + 1) * depth)

    sent = {}
    to_right, to_left = 2 * right + core, 2 * left + core
    for j in range(PIECES):
        jl = (j + PIECES // 2) % PIECES
        sent[j] = send(j, w_ref.at[piece(j), :], here, piece(j), to_right)
        sent[4 + jl] = send(4 + jl, w_ref.at[piece(jl), :], here, piece(jl), to_left)
    sent[8] = send(8, w_ref, here, slice(0, dim), mate)
    for c in loads:
        c.start()

    rows = seq // 2

    def finish(prod, slot, sl):
        cos, sin = cos_buf[sl, :], sin_buf[sl, :]
        cos, sin = jnp.concatenate([cos, cos], axis=1), jnp.concatenate([-sin, sin], axis=1)
        for n, dst in ((0, q_ref), (1, k_ref)):
            p = prod[:, n * hd:(n + 1) * hd].astype(BF16).astype(F32)
            dst[slot, sl, :] = (p * cos + pltpu.roll(p, hd // 2, 1) * sin).astype(BF16)
        v_ref[slot, sl, :] = prod[:, 2 * hd:].astype(BF16)

    def over(slots, fn):
        def body(i, carry):
            sl = pl.ds(pl.multiple_of(lax.rem(i, 2) * rows, rows), rows)
            fn(i // 2, jnp.where(i < 2, slots[0], slots[1]), sl)
            return carry

        lax.fori_loop(0, 4, body, 0)

    def part_of(slot, sl, j):
        return jnp.dot(u_buf[sl, piece(j)], w_buf[slot, piece(j), :], preferred_element_type=F32)

    def project(slots):
        over(slots, lambda n, slot, sl: finish(jnp.dot(u_buf[sl, :], w_buf[slot], preferred_element_type=F32), slot, sl))

    def project_first(slots):
        def fn(n, slot, sl):
            acc[n, sl, :] = part_of(slot, sl, 0) + part_of(slot, sl, 2)

        over(slots, fn)

    def project_last(slots):
        over(slots, lambda n, slot, sl: finish(acc[n, sl, :] + part_of(slot, sl, 1) + part_of(slot, sl, 3), slot, sl))

    stores = []

    def store(slot, i):
        cp = pltpu.make_async_copy(w_buf.at[slot], all_ref.at[slot], out_sem.at[i])
        cp.start()
        stores.append(cp)

    for c in loads:
        c.wait()
    norm_rows = 64
    gain = gain_buf[...].astype(F32).reshape(1, dim)

    def norm(i, carry):
        sl = pl.ds(pl.multiple_of(i * norm_rows, norm_rows), norm_rows)
        x = u_buf[sl, :].astype(F32)
        mean_sq = jnp.sum(x * x, axis=-1, keepdims=True) * (1.0 / dim)
        u_buf[sl, :] = (x * lax.rsqrt(mean_sq + NORM_EPS) * gain).astype(BF16)
        return carry

    lax.fori_loop(0, seq // norm_rows, norm, 0)
    sent[8].wait_recv()
    store(here, 0)
    store(mate, 1)
    project((here, mate))
    ls, rs, fs = to_left, to_right, 2 * far + core
    for j in (0, 1):
        sent[j].wait_recv()
        sent[9 + j] = send(9 + j, w_buf.at[ls, piece(j), :], ls, piece(j), to_right)
        sent[4 + 2 + j].wait_recv()
        sent[11 + j] = send(11 + j, w_buf.at[rs, piece(2 + j), :], rs, piece(2 + j), to_left)
    sent[13] = send(13, w_buf.at[ls, A, :], ls, A, mate)
    sent[14] = send(14, w_buf.at[rs, B, :], rs, B, mate)
    for j in (0, 1):
        sent[2 + j].wait_recv()
        sent[4 + j].wait_recv()
    sent[15] = send(15, w_buf.at[ls, B, :], ls, B, mate)
    sent[16] = send(16, w_buf.at[rs, A, :], rs, A, mate)
    store(ls, 2)
    store(rs, 3)
    project((ls, rs))
    for i in (13, 14, 15, 16):
        sent[i].wait_recv()
    store(2 * left + other, 4)
    store(2 * right + other, 5)
    project((2 * left + other, 2 * right + other))
    last = (fs, 2 * far + other)
    for j in (0, 1):
        sent[9 + j].wait_recv()
        sent[17 + 2 * j] = send(17 + 2 * j, w_buf.at[fs, piece(j), :], fs, piece(j), mate)
        sent[11 + j].wait_recv()
        sent[18 + 2 * j] = send(18 + 2 * j, w_buf.at[fs, piece(2 + j), :], fs, piece(2 + j), mate)
        sent[17 + 2 * j].wait_recv()
        sent[18 + 2 * j].wait_recv()
        if j == 0:
            project_first(last)
    store(last[0], 6)
    store(last[1], 7)
    project_last(last)
    for cp in sent.values():
        cp.wait_send()
    for cp in stores:
        cp.wait()


def gather_qkv_call(n, x, gain, w, cos, sin):
    seq, dim = x.shape
    packed = w.shape[1]
    hd = packed // 3
    act = jax.ShapeDtypeStruct((n, seq, hd), BF16)
    any_spec = pl.BlockSpec(memory_space=pl.ANY)
    vmem = pl.BlockSpec(memory_space=pltpu.VMEM)
    return pl.pallas_call(
        functools.partial(gather_qkv_kernel, n // 2),
        in_specs=[any_spec] * 5,
        out_specs=[vmem, vmem, vmem, any_spec],
        out_shape=[act, act, act, jax.ShapeDtypeStruct((n, dim, packed), BF16)],
        scratch_shapes=[
            pltpu.VMEM((seq, dim), BF16),
            pltpu.VMEM((n, dim, packed), BF16),
            pltpu.VMEM((dim,), BF16),
            pltpu.VMEM((seq, hd // 2), F32),
            pltpu.VMEM((seq, hd // 2), F32),
            pltpu.VMEM((2, seq, packed), F32),
            pltpu.SemaphoreType.DMA((5,)),
            pltpu.SemaphoreType.DMA((n,)),
            pltpu.SemaphoreType.DMA((21,)),
            pltpu.SemaphoreType.DMA((21,)),
        ],
        compiler_params=pltpu.CompilerParams(collective_id=3, has_side_effects=True, vmem_limit_bytes=62 << 20),
        cost_estimate=pl.CostEstimate(flops=120_000_000_000, bytes_accessed=4 * dim * n * packed, transcendentals=0),
        name="gather_qkv",
    )(x, gain, w, cos, sin)


def unpack_kernel(w_ref, wq_ref, wk_ref, wv_ref):
    hd = w_ref.shape[2] // 3
    for i in range(2):
        cols = slice(i * hd, (i + 1) * hd)
        wq_ref[:, cols] = w_ref[i, :, 0:hd]
        wk_ref[:, cols] = w_ref[i, :, hd:2 * hd]
        wv_ref[:, cols] = w_ref[i, :, 2 * hd:3 * hd]


def unpack_call(wg):
    heads, dim, packed = wg.shape
    hd = packed // 3
    block = dim // 2
    wout = jax.ShapeDtypeStruct((dim, heads * hd), BF16)
    w_spec = pl.BlockSpec((block, 2 * hd), lambda h, r: (r, h))
    return pl.pallas_call(
        unpack_kernel,
        grid=(heads // 2, dim // block),
        in_specs=[pl.BlockSpec((2, block, packed), lambda h, r: (h, r, 0))],
        out_specs=[w_spec, w_spec, w_spec],
        out_shape=[wout, wout, wout],
        compiler_params=pltpu.CompilerParams(vmem_limit_bytes=62 << 20),
        cost_estimate=pl.CostEstimate(flops=dim * heads * packed, bytes_accessed=4 * dim * heads * packed, transcendentals=0),
        name="unpack",
    )(wg)


def gate_up_kernel(u_ref, w_ref, m_ref, wg_ref, wu_ref):
    ff = wg_ref.shape[1]
    wg_ref[0] = w_ref[0, 0:ff, :]
    wu_ref[0] = w_ref[0, ff:2 * ff, :]
    seq = u_ref.shape[0]
    tile = 1024

    def part(j, carry):
        sl = pl.ds(pl.multiple_of(j * tile, tile), tile)
        both = lax.dot_general(w_ref[0], u_ref[sl, :], (((1,), (1,)), ((), ())), preferred_element_type=F32)
        gate = both[0:ff].astype(BF16).astype(F32)
        up = both[ff:2 * ff].astype(BF16).astype(F32)
        m_ref[0, :, sl] = (gate * jax.nn.sigmoid(gate) * up).astype(BF16)
        return carry

    lax.fori_loop(0, seq // tile, part, 0)


def gate_up_call(u, wg):
    seq, dim = u.shape
    blocks, rows, _ = wg.shape
    ff = rows // 2
    wout = jax.ShapeDtypeStruct((blocks, ff, dim), BF16)
    wspec = pl.BlockSpec((1, ff, dim), lambda h: (h, 0, 0))
    return pl.pallas_call(
        gate_up_kernel,
        grid=(blocks,),
        in_specs=[
            pl.BlockSpec((seq, dim), lambda h: (0, 0), pipeline_mode=pl.Buffered(1)),
            pl.BlockSpec((1, rows, dim), lambda h: (h, 0, 0)),
        ],
        out_specs=[pl.BlockSpec((1, ff, seq), lambda h: (h, 0, 0)), wspec, wspec],
        out_shape=[jax.ShapeDtypeStruct((blocks, ff, seq), BF16), wout, wout],
        compiler_params=pltpu.CompilerParams(vmem_limit_bytes=60 << 20),
        cost_estimate=pl.CostEstimate(flops=2 * seq * dim * blocks * rows, bytes_accessed=4 * dim * blocks * rows, transcendentals=seq * ff * blocks),
        name="gate_up",
    )(u, wg)


CHUNKS = 2
COPIES = 12


def sum_kernel(n, transposed, col0, *refs):
    if transposed:
        a_ref, w_ref, res_ref, out_ref, *scratch = refs
    else:
        len_ref, q_ref, k_ref, v_ref, gain_ref, w_ref, res_ref, out_ref, norm_ref, norm_buf, norm_sem, *scratch = refs
    a_buf, w_buf, res_buf, part, own, first, second, gath, in_sem, out_sem, send_sem, recv_sem = scratch
    me = lax.axis_index("tpa")
    right, left, far = lax.rem(me + 1, n), lax.rem(me + n - 1, n), lax.rem(me + 2, n)
    order = (far, right, left, me)
    shard, width = own.shape
    half = width // 2
    rows = shard // CHUNKS
    tile = w_buf.shape[2]
    tiles = w_buf.shape[0]

    loads = []
    if transposed:
        for s in range(n):
            span = pl.ds(pl.multiple_of(order[s] * shard, shard), shard)
            loads.append(pltpu.make_async_copy(a_ref.at[:, span], a_buf.at[s], in_sem.at[s]))
    wloads = [pltpu.make_async_copy(w_ref.at[:, t * tile:(t + 1) * tile], w_buf.at[t], in_sem.at[n + t]) for t in range(tiles)]
    mine = pl.ds(pl.multiple_of(me * shard, shard), shard)
    res_load = pltpu.make_async_copy(res_ref.at[mine, col0:col0 + width], res_buf, in_sem.at[n + tiles])
    for c in loads[:1] + wloads + loads[1:] + [res_load]:
        c.start()

    barrier = pltpu.get_barrier_semaphore()
    for peer in (left, right):
        pl.semaphore_signal(barrier, inc=1, device_id={"tpa": peer}, device_id_type=MESH)
    pl.semaphore_wait(barrier, 2)

    A, B = slice(0, half), slice(half, width)

    def span_of(c):
        return slice(c * rows, (c + 1) * rows)

    def send(c, i, src, dst, peer):
        cp = pltpu.make_async_remote_copy(src_ref=src, dst_ref=dst, send_sem=send_sem.at[c, i], recv_sem=recv_sem.at[c, i], device_id={"tpa": peer}, device_id_type=MESH)
        cp.start()
        return cp

    dims = (((0,), (0,)), ((), ())) if transposed else (((1,), (0,)), ((), ()))

    def ready(s):
        if transposed:
            loads[s].wait()
            return
        heads, _, hd = k_ref.shape
        base = pl.multiple_of(order[s] * shard, shard)
        length = len_ref[0]

        def head(h, carry):
            q = q_ref[h, pl.ds(base, shard), :]
            sc = lax.dot_general(q, k_ref[h], (((1,), (1,)), ((), ())), preferred_element_type=F32) * hd ** -0.5
            row = base + lax.broadcasted_iota(jnp.int32, sc.shape, 0)
            col = lax.broadcasted_iota(jnp.int32, sc.shape, 1)
            sc = jnp.where((col <= row) & (col < length), sc, MASK_VALUE)
            e = jnp.exp(sc - jnp.max(sc, axis=-1, keepdims=True))
            prob = (e * (1.0 / jnp.sum(e, axis=-1, keepdims=True))).astype(BF16)
            out = jnp.dot(prob, v_ref[h], preferred_element_type=F32).astype(BF16)
            a_buf[s, :, pl.ds(pl.multiple_of(h * hd, hd), hd)] = out
            return carry

        lax.fori_loop(0, heads, head, 0)

    def product(s, t):
        return lax.dot_general(a_buf[s], w_buf[t], dims, preferred_element_type=F32)

    def tile_loop(lo, hi, fn):
        def body(t, carry):
            fn(t, pl.ds(pl.multiple_of(t * tile, tile), tile))
            return carry

        lax.fori_loop(lo, hi, body, 0)

    def fill(s, lo, hi):
        def fn(t, cols):
            part[s, :, cols] = product(s, t).astype(BF16)

        tile_loop(lo, hi, fn)

    sent = {}
    mid, quarter = tiles // 2, tiles // 4
    ready(0)
    for part_no in (0, 2, 1, 3):
        for t in range(part_no * quarter, (part_no + 1) * quarter):
            wloads[t].wait()
        fill(0, part_no * quarter, (part_no + 1) * quarter)
        side, c = divmod(part_no, 2)
        wide = width // 4
        src = part.at[0, :, part_no * wide:(part_no + 1) * wide]
        dst = first.at[side, :, c * wide:(c + 1) * wide]
        sent[c, side] = send(c, side, src, dst, (right, left)[side])
    ready(1)
    fill(1, mid, tiles)
    for c in range(CHUNKS):
        r = span_of(c)
        sent[c, 2] = send(c, 2, part.at[1, r, B], second.at[0, r, B], right)
    ready(2)
    fill(2, 0, mid)
    for c in range(CHUNKS):
        r = span_of(c)
        sent[c, 3] = send(c, 3, part.at[2, r, A], second.at[1, r, A], left)
    fill(1, 0, mid)
    fill(2, mid, tiles)
    ready(3)
    res_load.wait()

    def mine_too(t, cols):
        own[:, cols] = res_buf[:, cols].astype(F32) + product(3, t)

    tile_loop(0, tiles, mine_too)

    for c in range(CHUNKS):
        r = span_of(c)
        if c == 0:
            sent[0, 0].wait_recv()
            sent[1, 0].wait_recv()
        part[1, r, A] = (part[1, r, A].astype(F32) + first[0, r, :].astype(F32)).astype(BF16)
        sent[c, 4] = send(c, 4, part.at[1, r, A], second.at[0, r, A], right)
        if c == 0:
            sent[0, 1].wait_recv()
            sent[1, 1].wait_recv()
        part[2, r, B] = (part[2, r, B].astype(F32) + first[1, r, :].astype(F32)).astype(BF16)
        sent[c, 5] = send(c, 5, part.at[2, r, B], second.at[1, r, B], left)

    stores = []

    def normed(c, slot, owner):
        if transposed:
            return
        gain = gain_ref[...].astype(F32).reshape(1, width)
        step = 16

        def body(i, carry):
            sl = pl.ds(pl.multiple_of(c * rows + i * step, step), step)
            x = gath[slot, sl, :].astype(F32)
            mean_sq = jnp.sum(x * x, axis=-1, keepdims=True) * (1.0 / width)
            norm_buf[slot, sl, :] = (x * lax.rsqrt(mean_sq + NORM_EPS) * gain).astype(BF16)
            return carry

        lax.fori_loop(0, rows // step, body, 0)
        dst = norm_ref.at[pl.ds(pl.multiple_of(owner * shard + c * rows, rows), rows), :]
        cp = pltpu.make_async_copy(norm_buf.at[slot, span_of(c), :], dst, norm_sem.at[c, slot])
        cp.start()
        stores.append(cp)

    def store(c, slot, owner, i, cols):
        r = span_of(c)
        dst = out_ref.at[pl.ds(pl.multiple_of(owner * shard + c * rows, rows), rows), cols]
        cp = pltpu.make_async_copy(gath.at[slot, r, cols], dst, out_sem.at[c, i])
        cp.start()
        stores.append(cp)

    for c in range(CHUNKS):
        r = span_of(c)
        for i in (2, 4, 3, 5):
            sent[c, i].wait_recv()
        total = own[r, :] + second[0, r, :].astype(F32) + second[1, r, :].astype(F32)
        gath[0, r, :] = total.astype(BF16)
        sent[c, 6] = send(c, 6, gath.at[0, r, A], gath.at[1, r, A], right)
        sent[c, 7] = send(c, 7, gath.at[0, r, B], gath.at[2, r, B], left)
        sent[c, 8] = send(c, 8, gath.at[0, r, B], gath.at[1, r, B], right)
        sent[c, 9] = send(c, 9, gath.at[0, r, A], gath.at[2, r, A], left)
        store(c, 0, me, 0, slice(0, width))
    for c in range(CHUNKS):
        normed(c, 0, me)
    for c in range(CHUNKS):
        r = span_of(c)
        sent[c, 6].wait_recv()
        sent[c, 10] = send(c, 10, gath.at[1, r, A], gath.at[3, r, A], right)
        sent[c, 7].wait_recv()
        sent[c, 11] = send(c, 11, gath.at[2, r, B], gath.at[3, r, B], left)
        store(c, 1, left, 1, A)
        store(c, 2, right, 2, B)
    for c in range(CHUNKS):
        sent[c, 8].wait_recv()
        store(c, 1, left, 3, B)
        normed(c, 1, left)
        sent[c, 9].wait_recv()
        store(c, 2, right, 4, A)
        normed(c, 2, right)
    for c in range(CHUNKS):
        sent[c, 10].wait_recv()
        store(c, 3, far, 5, A)
        sent[c, 11].wait_recv()
        store(c, 3, far, 6, B)
        normed(c, 3, far)
    for cp in sent.values():
        cp.wait_send()
    for cp in stores:
        cp.wait()


def sum_call(n, a, w, res, col0, cid, transposed):
    depth, width = w.shape
    seq = res.shape[0]
    shard = seq // n
    tile = 512
    tiles = width // tile
    assert CHUNKS == 2 and tiles % 4 == 0
    any_spec = pl.BlockSpec(memory_space=pl.ANY)
    a_shape = (n, depth, shard) if transposed else (n, shard, depth)
    vmem = pl.BlockSpec(memory_space=pltpu.VMEM)
    head_specs = [any_spec] if transposed else [pl.BlockSpec(memory_space=pltpu.SMEM), vmem, vmem, vmem, vmem]
    out = jax.ShapeDtypeStruct((seq, width), BF16)
    norm_scratch = [] if transposed else [pltpu.VMEM((4, shard, width), BF16), pltpu.SemaphoreType.DMA((CHUNKS, 4))]
    return pl.pallas_call(
        functools.partial(sum_kernel, n, transposed, col0),
        in_specs=head_specs + [any_spec] * 2,
        out_specs=any_spec if transposed else [any_spec] * 2,
        out_shape=out if transposed else [out] * 2,
        scratch_shapes=norm_scratch + [
            pltpu.VMEM(a_shape, BF16),
            pltpu.VMEM((tiles, depth, tile), BF16),
            pltpu.VMEM((shard, width), BF16),
            pltpu.VMEM((3, shard, width), BF16),
            pltpu.VMEM((shard, width), F32),
            pltpu.VMEM((2, shard, width // 2), BF16),
            pltpu.VMEM((2, shard, width), BF16),
            pltpu.VMEM((4, shard, width), BF16),
            pltpu.SemaphoreType.DMA((n + tiles + 1,)),
            pltpu.SemaphoreType.DMA((CHUNKS, 7)),
            pltpu.SemaphoreType.DMA((CHUNKS, COPIES)),
            pltpu.SemaphoreType.DMA((CHUNKS, COPIES)),
        ],
        compiler_params=pltpu.CompilerParams(collective_id=cid, has_side_effects=True, vmem_limit_bytes=62 << 20),
        cost_estimate=pl.CostEstimate(flops=2 * seq * depth * width + 130_000_000_000, bytes_accessed=2 * depth * width, transcendentals=0),
    )(*a, w, res)


def copy_kernel(src_ref, dst_ref):
    dst_ref[...] = src_ref[...]


def copy_call(w):
    rows, width = w.shape
    block = rows // 8
    spec = pl.BlockSpec((block, width), lambda i: (i, 0))
    return pl.pallas_call(
        copy_kernel,
        grid=(rows // block,),
        in_specs=[spec],
        out_specs=spec,
        out_shape=jax.ShapeDtypeStruct((rows, width), w.dtype),
        compiler_params=pltpu.CompilerParams(vmem_limit_bytes=62 << 20),
        cost_estimate=pl.CostEstimate(flops=rows * width, bytes_accessed=4 * rows * width, transcendentals=0),
    )(w)


def finish_kernel(ya_ref, yb_ref, da_ref, db_ref, y_ref, d_ref):
    half = ya_ref.shape[1]
    y_ref[:, :half] = ya_ref[...]
    y_ref[:, half:] = yb_ref[...]
    d_ref[:, :half] = da_ref[...]
    d_ref[:, half:] = db_ref[...]


def finish_call(y_a, y_b, d_a, d_b):
    steps = 8
    seq, half = y_a.shape
    ff = d_a.shape[0]

    def spec(rows, width):
        return pl.BlockSpec((rows // steps, width), lambda i: (i, 0))

    return pl.pallas_call(
        finish_kernel,
        grid=(steps,),
        in_specs=[spec(seq, half), spec(seq, half), spec(ff, half), spec(ff, half)],
        out_specs=[spec(seq, 2 * half), spec(ff, 2 * half)],
        out_shape=[jax.ShapeDtypeStruct((seq, 2 * half), BF16), jax.ShapeDtypeStruct((ff, 2 * half), BF16)],
        compiler_params=pltpu.CompilerParams(vmem_limit_bytes=62 << 20),
        cost_estimate=pl.CostEstimate(flops=ff * half, bytes_accessed=8 * (seq + ff) * half, transcendentals=0),
        name="finish",
    )(y_a, y_b, d_a, d_b)


def solution(mesh):
    n_tpa = mesh.shape['tpa']
    assert n_tpa == 4

    def gather(w, tiled):
        return lax.all_gather(w, 'tpb', axis=0, tiled=tiled)

    def layer(x_loc, len_loc, k_buf, v_buf, w_qkv, w_o, w_gate_up, w_down, g_attn, g_mlp):
        seq, dim = x_loc.shape[1:]
        _, hd = k_buf.shape[2:]
        half = dim // 2
        x = x_loc[0]
        cos, sin = rope_tables(seq, hd)
        o_g = gather(w_o, True)
        q, k, v, qkv_g = gather_qkv_call(mesh.shape['tpb'], x, g_attn, w_qkv, cos, sin)
        gu_in, d_in, q = lax.optimization_barrier((w_gate_up.T, w_down, q))
        gu_g = gather(gu_in, False)
        down_a = gather(d_in[:, :half], True)
        down_b = gather(d_in[:, half:], True)
        hidden, u2 = sum_call(n_tpa, (len_loc, q, k, v, g_mlp), o_g, x, 0, 0, False)

        hidden, u2, k, v, o_g, qkv_g = lax.optimization_barrier((hidden, u2, k, v, o_g, qkv_g))
        valid = (jnp.arange(seq) < len_loc[0])[:, None, None]
        k_cache = jnp.where(valid, k.transpose(1, 0, 2), k_buf[0])[None]
        v_cache = jnp.where(valid, v.transpose(1, 0, 2), v_buf[0])[None]
        o_out = copy_call(o_g)
        w_q, w_k, w_v = unpack_call(qkv_g)
        u2, k_cache, v_cache, o_out, w_q, w_k, w_v = lax.optimization_barrier((u2, k_cache, v_cache, o_out, w_q, w_k, w_v))
        m_t, gate_t, up_t = gate_up_call(u2, gu_g)
        ff = m_t.shape[0] * m_t.shape[1]
        m_t = m_t.reshape(ff, seq)
        y_a = sum_call(n_tpa, (m_t,), down_a, hidden, 0, 1, True)
        y_b = sum_call(n_tpa, (m_t,), down_b, hidden, half, 2, True)
        y, down = finish_call(y_a, y_b, down_a, down_b)
        return (y[None], k_cache, v_cache, w_q, w_k, w_v, o_out, gate_t.reshape(ff, dim).T, up_t.reshape(ff, dim).T, down)

    batch_spec = P(('part', 'tpb'), None, None)
    len_spec = P(('part', 'tpb'))
    cache_spec = P(('part', 'tpb'), None, 'tpa', None)
    train_cols = P('part', ('tpa', 'tpb'))
    train_rows = P(('part', 'tpa', 'tpb'), None)
    gain_spec = P('part')
    gen_cols = P('part', 'tpa')
    gen_rows = P(('part', 'tpa'), None)
    return jax.shard_map(layer, mesh=mesh, in_specs=(batch_spec, len_spec, cache_spec, cache_spec, train_cols, train_rows, train_cols, train_rows, gain_spec, gain_spec), out_specs=(batch_spec, cache_spec, cache_spec, gen_cols, gen_cols, gen_cols, gen_rows, gen_cols, gen_cols, gen_rows), check_vma=False)
```

time: 671 us -> 614 us (0.915)
  Pallas kernels: 426 us -> 566 us
  waiting for transfers between devices: 142 us -> 9.15 us
  other arithmetic: 70.3 us -> 7.65 us
    pallas_call x2 -> x3, Pallas kernels: 61 us -> 193 us  [the longest x1 152 us: gather_qkv_call(): pl.pallas_call(functools.partial(gather_qkv_kernel, n // 2), in_specs=[an...]
    all_gather x5 -> x4, waiting for transfers between devices: 139 us -> 8.23 us  [gather(): return lax.all_gather(w, 'tpb', axis=0, tiled=tiled)]
    convert_element_type x4 -> x0, other arithmetic: 22.7 us -> none  [the longest x2 22.1 us: rms_norm(): (x_wide * lax.rsqrt(mean_sq + NORM_EPS) * gain_vec.astype(F32)).astype(BF16)]
    concatenate x2 -> x0, other arithmetic: 21.3 us -> none  [the longest x1 20 us: layer(): down = jnp.concatenate([down_a, down_b], axis=1)]
    reduce_sum x2 -> x0, other arithmetic: 10.3 us -> none  [rms_norm(): mean_sq = jnp.mean(x_wide * x_wide, axis=-1, keepdims=True)]
    pallas_call x3, Pallas kernels: 297 us -> 305 us  [sum_call(): pl.pallas_call(functools.partial(sum_kernel, n, transposed, col0), in_spe...]
  transfers between devices with their start and end apart: 5 -> 4, of which waited for: 2 -> 2; matrix products, arithmetic and copies ran while one was open for 7% -> 2% of each run, Pallas kernels for 53% -> 77%
where the time goes in v2:
time: 614 us; the launch traced here: 607 us
  Pallas kernels  566 us (92%)
  between operations  14.7 us (2%)
  waiting for transfers between devices  9.15 us (1%)
  local copies, waits for them, and re-layouts  8.8 us (1%)
  other arithmetic  7.65 us (1%)
    pallas_call x3, Pallas kernels, sum_call(): pl.pallas_call(functools.partial(sum_kernel, n, transposed, col0), in_spe...  305 us
    pallas_call x1, Pallas kernels, gather_qkv_call(): pl.pallas_call(functools.partial(gather_qkv_kernel, n // 2), in_specs=[an...  152 us
    pallas_call x1, Pallas kernels, gate_up_call(): pl.pallas_call(gate_up_kernel, grid=(blocks,), in_specs=[pl.BlockSpec((se...  58.9 us
    pallas_call x1, Pallas kernels, finish_call(): pl.pallas_call(finish_kernel, grid=(steps,), in_specs=[spec(seq, half), s...  21.3 us
    pallas_call x1, Pallas kernels, unpack_call(): pl.pallas_call(unpack_kernel, grid=(heads // 2, dim // block), in_specs=[...  19.4 us
  transfers between devices with their start and end apart: 4, of which 2 were waited for; matrix products, arithmetic and copies ran while one was open for 2% of the time, Pallas kernels for 77%

profile of v2, /device:TPU:97, one launch (start us, length us, event | category | flops | bytes accessed | tf_op | source)
XLA Modules:
  0.0 607.3 jit_solution(5990330113638570218)
XLA Ops:
  7.2 0.1 all-gather.6.cloned.1.call-start
  7.3 0.7 all-gather.6.cloned.1.call-update
  8.0 0.1 all-gather.12.cloned.1.call-start
  8.1 2.8 fusion.2
  10.9 152.5 %gather_qkv.1 = (bf16[8,1024,128]{2,1,0:T(8,128)(2,1)}, bf16[8,1024,128]{2,1,0:T(8,128)(2,1)}, bf16[8,1024,128]{2,1,0:T(8,128)(2,1)}, bf16[8,4096,384]{2,1,0:T(8,128)(2,1)}) custom-call(bf16[1024,4096]{1,0:T(8,128)(2,1)} %bitcast.31, bf16[4096]{0:T(1024)(128)(2,1)} %gain_ref.1, bf16[4096,384]{1,0:T(8,128)(2,1)} %w_ref.1, ...), custom_call_target="tpu_custom_call" | custom-call | flops 120000004096 | bytes 50331648 | tf_op jit(solution)/shard_map/gather_qkv/pallas_call | solution.py:185
  163.4 0.0 copy-start
  163.4 0.1 all-gather.12.cloned.1.call-update
  163.4 0.1 all-gather.10.cloned.1.call-start
  163.5 1.7 copy-done
  165.2 1.8 fusion.4
  167.0 0.1 all-gather.10.cloned.1.call-update
  167.0 0.5 all-gather.8.cloned.1.call-start
  167.6 0.1 all-gather.8.cloned.1.call-update
  168.3 0.6 iota_compare_fusion
  168.9 0.0 all-gather.6.cloned.1.call-done.refs_5_.src_ref
  168.9 154.4 %shard_map.177 = (bf16[1024,4096]{1,0:T(8,128)(2,1)}, bf16[1024,4096]{1,0:T(8,128)(2,1)}) custom-call(s32[1]{0:T(128)} %copy.26.refs_0_, bf16[8,1024,128]{2,1,0:T(8,128)(2,1)} %get-tuple-element.41.refs_1_, bf16[8,1024,128]{2,1,0:T(8,128)(2,1)} %get-tuple-element.48.refs_2_, bf16[8,1024,128]{2,1,0:T(8,128)(2,1)} %get-tuple-element.49.refs_3_, ...), custom_call_target="tpu_custom_call" | custom-call | flops 138589929472 | bytes 8388608 | tf_op jit(solution)/shard_map/pallas_call | solution.py:485
  323.3 9.0 %shard_map.178 = bf16[1024,4096]{1,0:T(8,128)(2,1)} custom-call(bf16[1024,4096]{1,0:T(8,128)(2,1)} %all-gather.6.cloned.1.call-done.refs_5_.src_ref), custom_call_target="tpu_custom_call" | custom-call | flops 4194304 | bytes 16777216 | tf_op jit(solution)/shard_map/pallas_call | solution.py:517
  332.3 0.0 copy-start.1
  332.3 19.4 %unpack.1 = (bf16[4096,1024]{1,0:T(8,128)(2,1)}, bf16[4096,1024]{1,0:T(8,128)(2,1)}, bf16[4096,1024]{1,0:T(8,128)(2,1)}) custom-call(bf16[8,4096,384]{2,1,0:T(8,128)(2,1)} %get-tuple-element.51.w_ref), custom_call_target="tpu_custom_call" | custom-call | flops 12582912 | bytes 50331648 | tf_op jit(solution)/shard_map/unpack/pallas_call | solution.py:223
  351.7 0.0 copy-done.1
  351.7 4.3 fusion
  355.9 2.7 copy.22
  358.6 2.7 copy.23
  361.3 6.3 %all-gather.12.cloned.1.call-done = bf16[5504,4096]{1,0:T(8,128)(2,1)} async-done(((bf16[688,4096]{1,0:T(8,128)(2,1)}), bf16[5504,4096]{1,0:T(8,128)(2,1)}) %all-gather.12.cloned.1.call-update) | async-done | bytes 45088784 | tf_op jit(solution)/shard_map/all_gather | solution.py:561
  367.5 58.9 %gate_up.1 = (bf16[8,344,1024]{2,1,0:T(8,128)(2,1)}, bf16[8,344,4096]{2,1,0:T(8,128)(2,1)}, bf16[8,344,4096]{2,1,0:T(8,128)(2,1)}) custom-call(bf16[1024,4096]{1,0:T(8,128)(2,1)} %get-tuple-element.55.u_ref, bf16[8,688,4096]{2,1,0:T(8,128)(2,1)} %bitcast.30), custom_call_target="tpu_custom_call" | custom-call | flops 46170898432 | bytes 90177536 | tf_op jit(solution)/shard_map/gate_up/pallas_call | solution.py:259
  426.5 2.0 all-gather.10.cloned.1.call-done.refs_1_.db_ref
  428.4 75.7 %shard_map.180.yb_ref = bf16[1024,2048]{1,0:T(8,128)(2,1)} custom-call(bf16[2752,1024]{1,0:T(8,128)(2,1)} %bitcast.36, bf16[2752,2048]{1,0:T(8,128)(2,1)} %all-gather.10.cloned.1.call-done.refs_1_.db_ref, bf16[1024,4096]{1,0:T(8,128)(2,1)} %get-tuple-element.59.refs_2_), custom_call_target="tpu_custom_call" | custom-call | flops 141542719488 | bytes 11272192 | tf_op jit(solution)/shard_map/pallas_call | solution.py:485
  504.1 0.0 all-gather.8.cloned.1.call-done.refs_1_.da_ref
  504.1 75.1 %shard_map.179.ya_ref = bf16[1024,2048]{1,0:T(8,128)(2,1)} custom-call(bf16[2752,1024]{1,0:T(8,128)(2,1)} %bitcast.37, bf16[2752,2048]{1,0:T(8,128)(2,1)} %all-gather.8.cloned.1.call-done.refs_1_.da_ref, bf16[1024,4096]{1,0:T(8,128)(2,1)} %get-tuple-element.59.refs_2_), custom_call_target="tpu_custom_call" | custom-call | flops 141542719488 | bytes 11272192 | tf_op jit(solution)/shard_map/pallas_call | solution.py:485
  579.2 21.3 %finish.1 = (bf16[1024,4096]{1,0:T(8,128)(2,1)}, bf16[2752,4096]{1,0:T(8,128)(2,1)}) custom-call(bf16[1024,2048]{1,0:T(8,128)(2,1)} %shard_map.179.ya_ref, bf16[1024,2048]{1,0:T(8,128)(2,1)} %shard_map.180.yb_ref, bf16[2752,2048]{1,0:T(8,128)(2,1)} %all-gather.8.cloned.1.call-done.refs_1_.da_ref, bf16[2752,2048]{1,0:T(8,128)(2,1)} %all-gather.10.cloned.1.call-done.refs_1_.db_ref), custom_call_target="tpu_custom_call" | custom-call | flops 5636096 | bytes 61865984 | tf_op jit(solution)/shard_map/finish/pallas_call | solution.py:544
  (1 shorter events, 0.0 us)
Async XLA Ops:
  7.2 161.7 %all-gather.6.cloned.1.call-start = ((), (), s32[]{:S(2)}) async-start(), calls=%async_computation | async-start | bytes 9437184 | tf_op jit(solution)/shard_map/all_gather | solution.py:561
  8.0 359.6 %all-gather.12.cloned.1.call-start = ((), (), s32[]{:S(2)}) async-start(), calls=%async_computation.3 | async-start | bytes 50724864 | tf_op jit(solution)/shard_map/all_gather | solution.py:561
  163.4 1.8 copy-start
  163.4 265.0 %all-gather.10.cloned.1.call-start = ((), (), s32[]{:S(2)}) async-start(), calls=%async_computation.2 | async-start | bytes 12681216 | tf_op jit(solution)/shard_map/all_gather | solution.py:561
  167.0 337.1 %all-gather.8.cloned.1.call-start = ((), (), s32[]{:S(2)}) async-start(), calls=%async_computation.1 | async-start | bytes 12681216 | tf_op jit(solution)/shard_map/all_gather | solution.py:561
  332.3 19.4 %copy-start.1 = (pred[1024]{0:T(1024)(128)(4,1)S(1)}, pred[1024]{0:T(1024)(128)(4,1)}, u32[]{:S(2)}) copy-start(pred[1024]{0:T(1024)(128)(4,1)} %iota_compare_fusion) | copy-start | bytes 3076
Sparse Core Ops, SparseCore 0:
  9.6 85.2 all-gather.5
  163.6 203.9 all-gather.11
  369.7 58.6 all-gather.9
  429.9 59.5 all-gather.7

commit v3 on v2

--- a/solution.py
+++ b/solution.py
@@ -32,7 +32,7 @@
     return jnp.cos(angles), jnp.sin(angles)
 
 
-PIECES = 4
+PIECES = 8
 
 
 def gather_qkv_kernel(chips, x_ref, gain_ref, w_ref, cos_ref, sin_ref, q_ref, k_ref, v_ref, all_ref, u_buf, w_buf, gain_buf, cos_buf, sin_buf, acc, in_sem, out_sem, send_sem, recv_sem):
@@ -70,11 +70,13 @@
 
     sent = {}
     to_right, to_left = 2 * right + core, 2 * left + core
+    few = PIECES // 2
+    own_left, own_mate, on_right, on_left, sides, ends = PIECES, 2 * PIECES, 2 * PIECES + 1, 2 * PIECES + 1 + few, 3 * PIECES + 1, 3 * PIECES + 5
     for j in range(PIECES):
-        jl = (j + PIECES // 2) % PIECES
+        jl = (j + few) % PIECES
         sent[j] = send(j, w_ref.at[piece(j), :], here, piece(j), to_right)
-        sent[4 + jl] = send(4 + jl, w_ref.at[piece(jl), :], here, piece(jl), to_left)
-    sent[8] = send(8, w_ref, here, slice(0, dim), mate)
+        sent[own_left + jl] = send(own_left + jl, w_ref.at[piece(jl), :], here, piece(jl), to_left)
+    sent[own_mate] = send(own_mate, w_ref, here, slice(0, dim), mate)
     for c in loads:
         c.start()
 
@@ -102,14 +104,17 @@
     def project(slots):
         over(slots, lambda n, slot, sl: finish(jnp.dot(u_buf[sl, :], w_buf[slot], preferred_element_type=F32), slot, sl))
 
-    def project_first(slots):
+    def project_piece(slots, j):
         def fn(n, slot, sl):
-            acc[n, sl, :] = part_of(slot, sl, 0) + part_of(slot, sl, 2)
+            both = part_of(slot, sl, j) + part_of(slot, sl, j + few)
+            if j > 0:
+                both = acc[n, sl, :] + both
+            if j < few - 1:
+                acc[n, sl, :] = both
+            else:
+                finish(both, slot, sl)
 
         over(slots, fn)
-
-    def project_last(slots):
-        over(slots, lambda n, slot, sl: finish(acc[n, sl, :] + part_of(slot, sl, 1) + part_of(slot, sl, 3), slot, sl))
 
     stores = []
 
@@ -131,44 +136,44 @@
         return carry
 
     lax.fori_loop(0, seq // norm_rows, norm, 0)
-    sent[8].wait_recv()
+    sent[own_mate].wait_recv()
     store(here, 0)
     store(mate, 1)
     project((here, mate))
     ls, rs, fs = to_left, to_right, 2 * far + core
-    for j in (0, 1):
+    for j in range(few):
         sent[j].wait_recv()
-        sent[9 + j] = send(9 + j, w_buf.at[ls, piece(j), :], ls, piece(j), to_right)
-        sent[4 + 2 + j].wait_recv()
-        sent[11 + j] = send(11 + j, w_buf.at[rs, piece(2 + j), :], rs, piece(2 + j), to_left)
-    sent[13] = send(13, w_buf.at[ls, A, :], ls, A, mate)
-    sent[14] = send(14, w_buf.at[rs, B, :], rs, B, mate)
-    for j in (0, 1):
-        sent[2 + j].wait_recv()
-        sent[4 + j].wait_recv()
-    sent[15] = send(15, w_buf.at[ls, B, :], ls, B, mate)
-    sent[16] = send(16, w_buf.at[rs, A, :], rs, A, mate)
+        sent[on_right + j] = send(on_right + j, w_buf.at[ls, piece(j), :], ls, piece(j), to_right)
+        sent[own_left + few + j].wait_recv()
+        sent[on_left + j] = send(on_left + j, w_buf.at[rs, piece(few + j), :], rs, piece(few + j), to_left)
+    sent[sides] = send(sides, w_buf.at[ls, A, :], ls, A, mate)
+    sent[sides + 1] = send(sides + 1, w_buf.at[rs, B, :], rs, B, mate)
+    for j in range(few):
+        sent[few + j].wait_recv()
+        sent[own_left + j].wait_recv()
+    sent[sides + 2] = send(sides + 2, w_buf.at[ls, B, :], ls, B, mate)
+    sent[sides + 3] = send(sides + 3, w_buf.at[rs, A, :], rs, A, mate)
     store(ls, 2)
     store(rs, 3)
     project((ls, rs))
-    for i in (13, 14, 15, 16):
-        sent[i].wait_recv()
+    for i in range(4):
+        sent[sides + i].wait_recv()
     store(2 * left + other, 4)
     store(2 * right + other, 5)
     project((2 * left + other, 2 * right + other))
     last = (fs, 2 * far + other)
-    for j in (0, 1):
-        sent[9 + j].wait_recv()
-        sent[17 + 2 * j] = send(17 + 2 * j, w_buf.at[fs, piece(j), :], fs, piece(j), mate)
-        sent[11 + j].wait_recv()
-        sent[18 + 2 * j] = send(18 + 2 * j, w_buf.at[fs, piece(2 + j), :], fs, piece(2 + j), mate)
-        sent[17 + 2 * j].wait_recv()
-        sent[18 + 2 * j].wait_recv()
-        if j == 0:
-            project_first(last)
-    store(last[0], 6)
-    store(last[1], 7)
-    project_last(last)
+    for j in range(few):
+        a, b = ends + 2 * j, ends + 2 * j + 1
+        sent[on_right + j].wait_recv()
+        sent[a] = send(a, w_buf.at[fs, piece(j), :], fs, piece(j), mate)
+        sent[on_left + j].wait_recv()
+        sent[b] = send(b, w_buf.at[fs, piece(few + j), :], fs, piece(few + j), mate)
+        sent[a].wait_recv()
+        sent[b].wait_recv()
+        if j == few - 1:
+            store(last[0], 6)
+            store(last[1], 7)
+        project_piece(last, j)
     for cp in sent.values():
         cp.wait_send()
     for cp in stores:
@@ -196,8 +201,8 @@
             pltpu.VMEM((2, seq, packed), F32),
             pltpu.SemaphoreType.DMA((5,)),
             pltpu.SemaphoreType.DMA((n,)),
-            pltpu.SemaphoreType.DMA((21,)),
-            pltpu.SemaphoreType.DMA((21,)),
+            pltpu.SemaphoreType.DMA((4 * PIECES + 5,)),
+            pltpu.SemaphoreType.DMA((4 * PIECES + 5,)),
         ],
         compiler_params=pltpu.CompilerParams(collective_id=3, has_side_effects=True, vmem_limit_bytes=62 << 20),
         cost_estimate=pl.CostEstimate(flops=120_000_000_000, bytes_accessed=4 * dim * n * packed, transcendentals=0),
@@ -295,10 +300,13 @@
         for s in range(n):
             span = pl.ds(pl.multiple_of(order[s] * shard, shard), shard)
             loads.append(pltpu.make_async_copy(a_ref.at[:, span], a_buf.at[s], in_sem.at[s]))
-    wloads = [pltpu.make_async_copy(w_ref.at[:, t * tile:(t + 1) * tile], w_buf.at[t], in_sem.at[n + t]) for t in range(tiles)]
+
+    def wload(t):
+        return pltpu.make_async_copy(w_ref.at[:, pl.ds(pl.multiple_of(t * tile, tile), tile)], w_buf.at[t], in_sem.at[n + t])
+
     mine = pl.ds(pl.multiple_of(me * shard, shard), shard)
     res_load = pltpu.make_async_copy(res_ref.at[mine, col0:col0 + width], res_buf, in_sem.at[n + tiles])
-    for c in loads[:1] + wloads + loads[1:] + [res_load]:
+    for c in loads[:1] + [wload(t) for t in range(tiles)] + loads[1:] + [res_load]:
         c.start()
 
     barrier = pltpu.get_barrier_semaphore()
@@ -318,12 +326,9 @@
 
     dims = (((0,), (0,)), ((), ())) if transposed else (((1,), (0,)), ((), ()))
 
-    def ready(s):
-        if transposed:
-            loads[s].wait()
-            return
+    def ready(s, owner):
         heads, _, hd = k_ref.shape
-        base = pl.multiple_of(order[s] * shard, shard)
+        base = pl.multiple_of(owner * shard, shard)
         length = len_ref[0]
 
         def head(h, carry):
@@ -350,37 +355,79 @@
 
         lax.fori_loop(lo, hi, body, 0)
 
-    def fill(s, lo, hi):
+    sent = {}
+    mid, quarter, wide = tiles // 2, tiles // 4, width // 4
+
+    def far_copy(side, c, cols, start, peer):
+        return pltpu.make_async_remote_copy(src_ref=part.at[0, :, cols], dst_ref=first.at[side, :, pl.ds(start, wide)], send_sem=send_sem.at[c, side], recv_sem=recv_sem.at[c, side], device_id={"tpa": peer}, device_id_type=MESH)
+
+    if transposed:
+        loads[0].wait()
+    else:
+        ready(0, far)
+
+    def far_quarter(i, carry):
+        side, c = lax.rem(i, 2), i // 2
+        number = 2 * side + c
+
         def fn(t, cols):
-            part[s, :, cols] = product(s, t).astype(BF16)
-
-        tile_loop(lo, hi, fn)
-
-    sent = {}
-    mid, quarter = tiles // 2, tiles // 4
-    ready(0)
-    for part_no in (0, 2, 1, 3):
-        for t in range(part_no * quarter, (part_no + 1) * quarter):
-            wloads[t].wait()
-        fill(0, part_no * quarter, (part_no + 1) * quarter)
-        side, c = divmod(part_no, 2)
-        wide = width // 4
-        src = part.at[0, :, part_no * wide:(part_no + 1) * wide]
-        dst = first.at[side, :, c * wide:(c + 1) * wide]
-        sent[c, side] = send(c, side, src, dst, (right, left)[side])
-    ready(1)
-    fill(1, mid, tiles)
+            wload(t).wait()
+            part[0, :, cols] = product(0, t).astype(BF16)
+
+        tile_loop(number * quarter, (number + 1) * quarter, fn)
+        cols = pl.ds(pl.multiple_of(number * wide, wide), wide)
+        far_copy(side, c, cols, pl.multiple_of(c * wide, wide), jnp.where(side == 0, right, left)).start()
+        return carry
+
+    lax.fori_loop(0, 4, far_quarter, 0)
+    for c in range(2):
+        for side in range(2):
+            number = 2 * side + c
+            sent[c, side] = far_copy(side, c, slice(number * wide, (number + 1) * wide), c * wide, (right, left)[side])
+
+    if transposed:
+        loads[1].wait()
+        loads[2].wait()
+    else:
+        def beside(s, carry):
+            ready(s, jnp.where(s == 1, right, left))
+            return carry
+
+        lax.fori_loop(1, 3, beside, 0)
+
+    def beside_tiles(i, carry):
+        turn, job = i // tiles, lax.rem(i, tiles)
+        s = 1 + job // mid
+        t = lax.rem(job, mid) + mid * lax.rem(s + turn, 2)
+        part[s, :, pl.ds(pl.multiple_of(t * tile, tile), tile)] = product(s, t).astype(BF16)
+
+        @pl.when(i == mid - 1)
+        def _():
+            direct(2)
+
+        @pl.when(i == tiles - 1)
+        def _():
+            direct(3)
+
+        return carry
+
+    def direct_copy(c, i):
+        r = span_of(c)
+        src, dst, peer = (part.at[1, r, B], second.at[0, r, B], right) if i == 2 else (part.at[2, r, A], second.at[1, r, A], left)
+        return pltpu.make_async_remote_copy(src_ref=src, dst_ref=dst, send_sem=send_sem.at[c, i], recv_sem=recv_sem.at[c, i], device_id={"tpa": peer}, device_id_type=MESH)
+
+    def direct(i):
+        for c in range(CHUNKS):
+            direct_copy(c, i).start()
+
+    lax.fori_loop(0, 2 * tiles, beside_tiles, 0)
     for c in range(CHUNKS):
-        r = span_of(c)
-        sent[c, 2] = send(c, 2, part.at[1, r, B], second.at[0, r, B], right)
-    ready(2)
-    fill(2, 0, mid)
-    for c in range(CHUNKS):
-        r = span_of(c)
-        sent[c, 3] = send(c, 3, part.at[2, r, A], second.at[1, r, A], left)
-    fill(1, 0, mid)
-    fill(2, mid, tiles)
-    ready(3)
+        for i in (2, 3):
+            sent[c, i] = direct_copy(c, i)
+    if transposed:
+        loads[3].wait()
+    else:
+        ready(3, me)
     res_load.wait()
 
     def mine_too(t, cols):

time: 614 us -> 607 us (0.989); the launches traced: 607 us -> 607 us
  transfers between devices with their start and end apart: 4 -> 4, of which waited for: 2 -> 2; matrix products, arithmetic and copies ran while one was open for 2% -> 2% of each run, Pallas kernels for 77% -> 76%
where the time goes in v3:
time: 607 us
  Pallas kernels  560 us (92%)
  waiting for transfers between devices  15.1 us (2%)
  between operations  14.5 us (2%)
  local copies, waits for them, and re-layouts  8.8 us (1%)
  other arithmetic  7.65 us (1%)
    pallas_call x3, Pallas kernels, sum_call(): pl.pallas_call(functools.partial(sum_kernel, n, transposed, col0), in_spe...  302 us
    pallas_call x1, Pallas kernels, gather_qkv_call(): pl.pallas_call(functools.partial(gather_qkv_kernel, n // 2), in_specs=[an...  150 us
    pallas_call x1, Pallas kernels, gate_up_call(): pl.pallas_call(gate_up_kernel, grid=(blocks,), in_specs=[pl.BlockSpec((se...  58.8 us
    pallas_call x1, Pallas kernels, finish_call(): pl.pallas_call(finish_kernel, grid=(steps,), in_specs=[spec(seq, half), s...  21.3 us
    pallas_call x1, Pallas kernels, unpack_call(): pl.pallas_call(unpack_kernel, grid=(heads // 2, dim // block), in_specs=[...  19.3 us
    all_gather x4, waiting for transfers between devices, gather(): return lax.all_gather(w, 'tpb', axis=0, tiled=tiled)  13.9 us
  transfers between devices with their start and end apart: 4, of which 2 were waited for; matrix products, arithmetic and copies ran while one was open for 2% of the time, Pallas kernels for 76%

profile of v3, /device:TPU:97, one launch (start us, length us, event | category | flops | bytes accessed | tf_op | source)
XLA Modules:
  0.0 606.8 jit_solution(12484619113608995830)
XLA Ops:
  7.2 0.1 all-gather.6.cloned.1.call-start
  7.3 0.7 all-gather.6.cloned.1.call-update
  8.0 0.1 all-gather.12.cloned.1.call-start
  8.1 2.8 fusion.2
  10.9 149.6 %gather_qkv.1 = (bf16[8,1024,128]{2,1,0:T(8,128)(2,1)}, bf16[8,1024,128]{2,1,0:T(8,128)(2,1)}, bf16[8,1024,128]{2,1,0:T(8,128)(2,1)}, bf16[8,4096,384]{2,1,0:T(8,128)(2,1)}) custom-call(bf16[1024,4096]{1,0:T(8,128)(2,1)} %bitcast.31, bf16[4096]{0:T(1024)(128)(2,1)} %gain_ref.1, bf16[4096,384]{1,0:T(8,128)(2,1)} %w_ref.1, ...), custom_call_target="tpu_custom_call" | custom-call | flops 120000004096 | bytes 50331648 | tf_op jit(solution)/shard_map/gather_qkv/pallas_call | solution.py:190
  160.5 0.0 copy-start
  160.5 0.1 all-gather.12.cloned.1.call-update
  160.6 0.1 all-gather.10.cloned.1.call-start
  160.6 1.7 copy-done
  162.3 1.8 fusion.4
  164.1 0.1 all-gather.10.cloned.1.call-update
  164.1 0.2 all-gather.8.cloned.1.call-start
  164.4 0.4 all-gather.8.cloned.1.call-update
  165.4 0.6 iota_compare_fusion
  166.0 0.0 all-gather.6.cloned.1.call-done.refs_5_.src_ref
  166.0 151.6 %shard_map.177 = (bf16[1024,4096]{1,0:T(8,128)(2,1)}, bf16[1024,4096]{1,0:T(8,128)(2,1)}) custom-call(s32[1]{0:T(128)} %copy.26.refs_0_, bf16[8,1024,128]{2,1,0:T(8,128)(2,1)} %get-tuple-element.41.refs_1_, bf16[8,1024,128]{2,1,0:T(8,128)(2,1)} %get-tuple-element.48.refs_2_, bf16[8,1024,128]{2,1,0:T(8,128)(2,1)} %get-tuple-element.49.refs_3_, ...), custom_call_target="tpu_custom_call" | custom-call | flops 138589929472 | bytes 8388608 | tf_op jit(solution)/shard_map/pallas_call | solution.py:532
  317.6 9.0 %shard_map.178 = bf16[1024,4096]{1,0:T(8,128)(2,1)} custom-call(bf16[1024,4096]{1,0:T(8,128)(2,1)} %all-gather.6.cloned.1.call-done.refs_5_.src_ref), custom_call_target="tpu_custom_call" | custom-call | flops 4194304 | bytes 16777216 | tf_op jit(solution)/shard_map/pallas_call | solution.py:564
  326.6 0.0 copy-start.1
  326.6 19.3 %unpack.1 = (bf16[4096,1024]{1,0:T(8,128)(2,1)}, bf16[4096,1024]{1,0:T(8,128)(2,1)}, bf16[4096,1024]{1,0:T(8,128)(2,1)}) custom-call(bf16[8,4096,384]{2,1,0:T(8,128)(2,1)} %get-tuple-element.51.w_ref), custom_call_target="tpu_custom_call" | custom-call | flops 12582912 | bytes 50331648 | tf_op jit(solution)/shard_map/unpack/pallas_call | solution.py:228
  345.9 0.0 copy-done.1
  345.9 4.3 fusion
  350.2 2.7 copy.22
  352.9 2.7 copy.23
  355.5 11.7 %all-gather.12.cloned.1.call-done = bf16[5504,4096]{1,0:T(8,128)(2,1)} async-done(((bf16[688,4096]{1,0:T(8,128)(2,1)}), bf16[5504,4096]{1,0:T(8,128)(2,1)}) %all-gather.12.cloned.1.call-update) | async-done | bytes 45088784 | tf_op jit(solution)/shard_map/all_gather | solution.py:608
  367.3 58.8 %gate_up.1 = (bf16[8,344,1024]{2,1,0:T(8,128)(2,1)}, bf16[8,344,4096]{2,1,0:T(8,128)(2,1)}, bf16[8,344,4096]{2,1,0:T(8,128)(2,1)}) custom-call(bf16[1024,4096]{1,0:T(8,128)(2,1)} %get-tuple-element.55.u_ref, bf16[8,688,4096]{2,1,0:T(8,128)(2,1)} %bitcast.30), custom_call_target="tpu_custom_call" | custom-call | flops 46170898432 | bytes 90177536 | tf_op jit(solution)/shard_map/gate_up/pallas_call | solution.py:264
  426.0 2.1 all-gather.10.cloned.1.call-done.refs_1_.db_ref
  428.2 75.7 %shard_map.180.yb_ref = bf16[1024,2048]{1,0:T(8,128)(2,1)} custom-call(bf16[2752,1024]{1,0:T(8,128)(2,1)} %bitcast.36, bf16[2752,2048]{1,0:T(8,128)(2,1)} %all-gather.10.cloned.1.call-done.refs_1_.db_ref, bf16[1024,4096]{1,0:T(8,128)(2,1)} %get-tuple-element.59.refs_2_), custom_call_target="tpu_custom_call" | custom-call | flops 141542719488 | bytes 11272192 | tf_op jit(solution)/shard_map/pallas_call | solution.py:532
  503.8 0.0 all-gather.8.cloned.1.call-done.refs_1_.da_ref
  503.9 75.1 %shard_map.179.ya_ref = bf16[1024,2048]{1,0:T(8,128)(2,1)} custom-call(bf16[2752,1024]{1,0:T(8,128)(2,1)} %bitcast.37, bf16[2752,2048]{1,0:T(8,128)(2,1)} %all-gather.8.cloned.1.call-done.refs_1_.da_ref, bf16[1024,4096]{1,0:T(8,128)(2,1)} %get-tuple-element.59.refs_2_), custom_call_target="tpu_custom_call" | custom-call | flops 141542719488 | bytes 11272192 | tf_op jit(solution)/shard_map/pallas_call | solution.py:532
  579.0 21.3 %finish.1 = (bf16[1024,4096]{1,0:T(8,128)(2,1)}, bf16[2752,4096]{1,0:T(8,128)(2,1)}) custom-call(bf16[1024,2048]{1,0:T(8,128)(2,1)} %shard_map.179.ya_ref, bf16[1024,2048]{1,0:T(8,128)(2,1)} %shard_map.180.yb_ref, bf16[2752,2048]{1,0:T(8,128)(2,1)} %all-gather.8.cloned.1.call-done.refs_1_.da_ref, bf16[2752,2048]{1,0:T(8,128)(2,1)} %all-gather.10.cloned.1.call-done.refs_1_.db_ref), custom_call_target="tpu_custom_call" | custom-call | flops 5636096 | bytes 61865984 | tf_op jit(solution)/shard_map/finish/pallas_call | solution.py:591
  (1 shorter events, 0.0 us)
Async XLA Ops:
  7.2 158.8 %all-gather.6.cloned.1.call-start = ((), (), s32[]{:S(2)}) async-start(), calls=%async_computation | async-start | bytes 9437184 | tf_op jit(solution)/shard_map/all_gather | solution.py:608
  8.0 359.3 %all-gather.12.cloned.1.call-start = ((), (), s32[]{:S(2)}) async-start(), calls=%async_computation.3 | async-start | bytes 50724864 | tf_op jit(solution)/shard_map/all_gather | solution.py:608
  160.5 1.8 copy-start
  160.6 267.6 %all-gather.10.cloned.1.call-start = ((), (), s32[]{:S(2)}) async-start(), calls=%async_computation.2 | async-start | bytes 12681216 | tf_op jit(solution)/shard_map/all_gather | solution.py:608
  164.1 339.7 %all-gather.8.cloned.1.call-start = ((), (), s32[]{:S(2)}) async-start(), calls=%async_computation.1 | async-start | bytes 12681216 | tf_op jit(solution)/shard_map/all_gather | solution.py:608
  326.6 19.4 %copy-start.1 = (pred[1024]{0:T(1024)(128)(4,1)S(1)}, pred[1024]{0:T(1024)(128)(4,1)}, u32[]{:S(2)}) copy-start(pred[1024]{0:T(1024)(128)(4,1)} %iota_compare_fusion) | copy-start | bytes 3076
Sparse Core Ops, SparseCore 0:
  9.6 85.2 all-gather.5
  160.7 206.5 all-gather.11
  369.5 58.6 all-gather.9
  429.6 59.5 all-gather.7
